TPU v7x, 32 devices: a whole 2x2x4 slice. The times are simulated.
32 devices in a mesh: rep: 2 (over x), dp: 16 (over y, z, core).
Axes of the slice: x: 2, y: 2, z: 4, core: 2. Of those that a mesh axis runs over, the one named last changes fastest.
Arguments:
- x: bfloat16 [32, 1024, 896], P(('rep', 'dp')), parts along dimension 0
- dy: bfloat16 [32, 1024, 896], P(('rep', 'dp')), parts along dimension 0
- w_gate: bfloat16 [2, 896, 4736], P(None, 'dp')
- w_up: bfloat16 [2, 896, 4736], P(None, 'dp')
- w_down: bfloat16 [2, 4736, 896], P(None, 'dp')
Outputs:
- output 1: bfloat16 [32, 1024, 896], P(('rep', 'dp')), parts along dimension 0
- output 2: bfloat16 [4, 896, 4736], P('rep', 'dp'), parts along dimension 0
- output 3: bfloat16 [4, 896, 4736], P('rep', 'dp'), parts along dimension 0
- output 4: bfloat16 [4, 4736, 896], P('rep', 'dp'), parts along dimension 0
There are 2 independent parts. A program takes and returns all parts, laid end to end along the dimension named above; an argument that names none is the same for every part.
All inputs are finite; a program needn't handle non-finite values.
Results may differ from a plain program's by a relative error of at most 0.018.
Values are sent between devices in bfloat16 or wider.
A program may use at most 2 GiB of HBM per device.

v0:
```python
import jax
import jax.numpy as jnp
from jax import lax

NAMES = ("w_gate", "w_up", "w_down")


def matmul(a, w):
    return jnp.dot(a, w, preferred_element_type=jnp.float32).astype(jnp.bfloat16)


def normed(h):
    wide = h.astype(jnp.float32)
    scale = lax.rsqrt(jnp.mean(wide**2, -1, keepdims=True) + 1e-6)
    return (wide * scale).astype(jnp.bfloat16)


def layer(h, w):
    a = normed(h)
    gate = jnp.dot(a, w["w_gate"], preferred_element_type=jnp.float32)
    up = jnp.dot(a, w["w_up"], preferred_element_type=jnp.float32)
    return h + matmul((jax.nn.silu(gate) * up).astype(jnp.bfloat16), w["w_down"])


def stack(weights, h):
    for number in range(weights["w_gate"].shape[0]):
        h = layer(h, {name: w[number] for name, w in weights.items()})
    return h


def solution(mesh):
    groups = mesh.shape["rep"]

    def step(x, dy, *weights):
        shape = x.shape
        x, dy = (t.reshape(groups, -1, *t.shape[1:]) for t in (x, dy))

        def of_a_group(x, dy):
            _, back = jax.vjp(stack, dict(zip(NAMES, weights, strict=True)), x)
            by_weights, by_x = back(dy)
            return (by_x, *(by_weights[name] for name in NAMES))

        by_x, *by_weights = jax.vmap(of_a_group)(x, dy)
        return (by_x.reshape(shape), *(t.reshape(-1, *t.shape[2:]) for t in by_weights))

    return step
```

profile of v0, /device:TPU:0, one launch (start us, length us, event | category | flops | bytes accessed | tf_op | source)
XLA Modules:
  0.0 1643.6 jit_solution(7026123592573005675)
XLA Ops:
  7.2 2.4 fusion.96
  9.7 2.3 fusion.97
  11.9 0.0 all-gather.34.cloned.1.call-start
  12.0 2.3 fusion.98
  14.4 0.5 all-gather.38.cloned.1.call-update
  14.9 0.5 all-gather.36.cloned.1.call-update
  15.5 0.5 all-gather.40.cloned.1.call-update
  16.1 2.4 copy.1
  18.5 3.8 copy
  22.3 0.4 fusion.55
  22.8 0.6 multiply_add_fusion.1
  23.4 65.4 %all-gather.32.cloned.1.call-done = bf16[1,896,4736]{2,1,0:T(8,128)(2,1)} async-done(((bf16[1,56,4736]{2,1,0:T(8,128)(2,1)}), bf16[1,896,4736]{2,1,0:T(8,128)(2,1)}) %all-gather.32.cloned.1.call-update) | async-done | bytes 8486928 | tf_op jit(solution)/vmap(jvp())/squeeze | solution.py:27
  88.7 17.3 %fusion.49 = f32[1024,4736]{1,0:T(8,128)} fusion(bf16[1,896,4736]{2,1,0:T(8,128)(2,1)} %all-gather.32.cloned.1.call-done, bf16[1,1024,896]{2,1,0:T(8,128)(2,1)S(1)} %copy-done.3, f32[1024]{0:T(1024)S(1)} %get-tuple-element.13), kind=kOutput, calls=%fused_computation.60 | convolution fusion | flops 8693350400 | bytes 29724672 | tf_op jit(solution)/vmap(jvp())/dot_general | solution.py:21
  106.0 58.3 %all-gather.30.cloned.1.call-done = bf16[1,896,4736]{2,1,0:T(8,128)(2,1)} async-done(((bf16[1,56,4736]{2,1,0:T(8,128)(2,1)}), bf16[1,896,4736]{2,1,0:T(8,128)(2,1)}) %all-gather.30.cloned.1.call-update) | async-done | bytes 8486928 | tf_op jit(solution)/vmap(jvp())/squeeze | solution.py:27
  164.3 13.5 fusion.53
  177.9 6.5 copy-done
  184.4 14.0 fusion.30
  198.3 41.6 %all-gather.34.cloned.1.call-done = bf16[1,4736,896]{2,1,0:T(8,128)(2,1)} async-done(((bf16[1,296,896]{2,1,0:T(8,128)(2,1)}), bf16[1,4736,896]{2,1,0:T(8,128)(2,1)}) %all-gather.34.cloned.1.call-update) | async-done | bytes 8486928 | tf_op jit(solution)/vmap(jvp())/squeeze | solution.py:27
  240.0 15.6 fusion.63
  255.6 59.8 %all-gather.38.cloned.1.call-done = bf16[1,4736,896]{2,1,0:T(8,128)(2,1)} async-done(((bf16[1,296,896]{2,1,0:T(8,128)(2,1)}), bf16[1,4736,896]{2,1,0:T(8,128)(2,1)}) %all-gather.38.cloned.1.call-update) | async-done | bytes 8486928 | tf_op jit(solution)/vmap(jvp())/squeeze | solution.py:27
  315.4 16.6 %convolution_convert_fusion.1 = bf16[1024,4736]{1,0:T(8,128)(2,1)} fusion(bf16[1,4736,896]{2,1,0:T(8,128)(2,1)} %all-gather.38.cloned.1.call-done, bf16[1,1024,896]{2,1,0:T(8,128)(2,1)} %param), kind=kOutput, calls=%fused_computation.47 | convolution fusion | flops 8695447552 | bytes 20021248 | tf_op jit(solution)/vmap(transpose(jvp()))/dot_general | solution.py:9
  332.0 59.5 %all-gather.36.cloned.1.call-done = bf16[1,896,4736]{2,1,0:T(8,128)(2,1)} async-done(((bf16[1,56,4736]{2,1,0:T(8,128)(2,1)}), bf16[1,896,4736]{2,1,0:T(8,128)(2,1)}) %all-gather.36.cloned.1.call-update) | async-done | bytes 8486928 | tf_op jit(solution)/vmap(jvp())/squeeze | solution.py:27
  391.5 16.7 %fusion.43 = f32[1024,4736]{1,0:T(8,128)} fusion(bf16[1,896,4736]{2,1,0:T(8,128)(2,1)} %all-gather.36.cloned.1.call-done, bf16[1,1,1024,896]{2,3,1,0:T(8,128)(2,1)S(1)} %copy-done.9, f32[1024]{0:T(1024)S(1)} %bitcast.262), kind=kOutput, calls=%fused_computation.54 | convolution fusion | flops 8693350400 | bytes 29724672 | tf_op jit(solution)/vmap(jvp())/dot_general | solution.py:20
  408.2 59.3 %all-gather.40.cloned.1.call-done = bf16[1,896,4736]{2,1,0:T(8,128)(2,1)} async-done(((bf16[1,56,4736]{2,1,0:T(8,128)(2,1)}), bf16[1,896,4736]{2,1,0:T(8,128)(2,1)}) %all-gather.40.cloned.1.call-update) | async-done | bytes 8486928 | tf_op jit(solution)/vmap(jvp())/squeeze | solution.py:27
  467.5 17.3 %fusion.37 = f32[1024,4736]{1,0:T(8,128)} fusion(bf16[1,896,4736]{2,1,0:T(8,128)(2,1)} %all-gather.40.cloned.1.call-done, bf16[1,1,1024,896]{2,3,1,0:T(8,128)(2,1)S(1)} %copy-done.9, f32[1024]{0:T(1024)S(1)} %bitcast.263), kind=kOutput, calls=%fused_computation.48 | convolution fusion | flops 8693350400 | bytes 29724672 | tf_op jit(solution)/vmap(jvp())/dot_general | solution.py:21
  484.9 17.1 %fusion.4 = bf16[1024,4736]{1,0:T(8,128)(2,1)} fusion(f32[1024,4736]{1,0:T(8,128)S(1)} %copy-done.1, f32[1024,4736]{1,0:T(8,128)} %fusion.37, bf16[1024,4736]{1,0:T(8,128)(2,1)} %convolution_convert_fusion.1), kind=kLoop, calls=%fused_computation.10 | loop fusion | flops 58195968 | bytes 58195968
  502.0 18.3 %fusion.22 = bf16[1024,896]{0,1:T(8,128)(2,1)} fusion(bf16[1024,4736]{1,0:T(8,128)(2,1)} %convolution_convert_fusion.1, f32[1024,4736]{1,0:T(8,128)} %fusion.43, bf16[1,896,4736]{2,1,0:T(8,128)(2,1)} %all-gather.40.cloned.1.call-done), kind=kOutput, calls=%fused_computation.33 | convolution fusion | flops 8719695872 | bytes 39419904 | tf_op jit(solution)/vmap(transpose(jvp()))/dot_general | solution.py:21
  520.3 15.4 fusion.65
  535.8 1.3 fusion.70
  537.1 1.2 copy-done.8
  538.4 13.0 convolution_bitcast_fusion.2
  551.4 0.0 reduce-scatter.33.cloned.1.call-start
  551.5 14.6 convolution_convert_fusion
  566.1 3.7 copy-done.2
  569.8 18.9 %fusion.7 = bf16[1024,4736]{1,0:T(8,128)(2,1)} fusion(f32[1024,4736]{1,0:T(8,128)} %copy-done, f32[1024,4736]{1,0:T(8,128)} %fusion.49, bf16[1024,4736]{1,0:T(8,128)(2,1)S(1)} %convolution_convert_fusion), kind=kLoop, calls=%fused_computation.13 | loop fusion | flops 58195968 | bytes 58195968
  588.8 18.3 %fusion.18 = bf16[1024,896]{0,1:T(8,128)(2,1)} fusion(bf16[1024,4736]{1,0:T(8,128)(2,1)} %copy-done.2, f32[1024,4736]{1,0:T(8,128)} %copy-done, bf16[1,896,4736]{2,1,0:T(8,128)(2,1)} %all-gather.32.cloned.1.call-done), kind=kOutput, calls=%fused_computation.31 | convolution fusion | flops 8719695872 | bytes 39419904 | tf_op jit(solution)/vmap(transpose(jvp()))/dot_general | solution.py:21
  607.1 16.5 %fusion.61 = (f32[1024]{0:T(1024)S(1)}, bf16[1024,896]{0,1:T(8,128)(2,1)}) fusion(bf16[1,1024,896]{1,2,0:T(8,128)(2,1)} %copy.1, bf16[1024,896]{0,1:T(8,128)(2,1)} %fusion.18, bf16[1024,4736]{1,0:T(8,128)(2,1)} %fusion.7, bf16[1,896,4736]{2,1,0:T(8,128)(2,1)} %all-gather.30.cloned.1.call-done), kind=kOutput, calls=%fused_computation.83 | convolution fusion | flops 8695184384 | bytes 23695360 | tf_op jit(solution)/vmap(transpose(jvp()))/dot_general | solution.py:20
  623.6 0.6 fusion.99
  624.3 11.9 convolution_bitcast_fusion
  636.2 0.0 reduce-scatter.31.cloned.1.call-start
  636.2 1.4 copy-done.11
  637.7 15.5 convolution_bitcast_fusion.1
  653.2 1.4 copy-done.6
  654.7 18.7 %fusion.27 = f32[1,896,4736]{2,1,0:T(8,128)} fusion(bf16[1024,4736]{1,0:T(8,128)(2,1)} %copy-done.2, f32[1024,4736]{1,0:T(8,128)} %copy-done, bf16[1,1024,896]{1,2,0:T(8,128)(2,1)S(1)} %copy-done.6, f32[1024]{0:T(1024)S(1)} %bitcast.268), kind=kOutput, calls=%fused_computation.35 | convolution fusion | flops 8722448384 | bytes 47910912 | tf_op jit(solution)/vmap(transpose(jvp()))/dot_general | solution.py:21
  673.4 19.6 %fusion.24 = f32[1,896,4736]{2,1,0:T(8,128)} fusion(bf16[1024,4736]{1,0:T(8,128)(2,1)} %convolution_convert_fusion.1, f32[1024,4736]{1,0:T(8,128)} %fusion.43, bf16[1,1,1024,896]{2,3,1,0:T(8,128)(2,1)} %get-tuple-element.15, f32[1024]{0:T(1024)S(1)} %bitcast.266), kind=kOutput, calls=%fused_computation.34 | convolution fusion | flops 8722448384 | bytes 47910912 | tf_op jit(solution)/vmap(transpose(jvp()))/dot_general | solution.py:21
  693.1 24.3 %convolution_bitcast_fusion.3 = f32[1,4736,896]{2,1,0:T(8,128)} fusion(f32[1024,4736]{1,0:T(8,128)} %fusion.37, f32[1024,4736]{1,0:T(8,128)} %fusion.43, bf16[1,1024,896]{2,1,0:T(8,128)(2,1)} %param), kind=kOutput, calls=%fused_computation.39 | convolution fusion | flops 8719695872 | bytes 57606144 | tf_op jit(solution)/vmap(transpose(jvp()))/dot_general | solution.py:9
  717.3 0.7 copy-done.12
  718.0 4.6 fusion.69
  722.6 3.8 copy.2
  726.4 1.4 reduce-scatter.41.cloned.1.call-done
  727.8 1.3 convert_bitcast_fusion
  729.1 180.0 %reduce-scatter.33.cloned.1.call-done = f32[1,56,4736]{2,1,0:T(8,128)} async-done(((f32[1,896,4736]{2,1,0:T(8,128)}), f32[1,56,4736]{2,1,0:T(8,128)}) %reduce-scatter.33.cloned.1.call-update) | async-done | bytes 1060880
  909.1 1.3 convert_bitcast_fusion.4
  910.4 180.0 %reduce-scatter.31.cloned.1.call-done = f32[1,56,4736]{2,1,0:T(8,128)} async-done(((f32[1,896,4736]{2,1,0:T(8,128)}), f32[1,56,4736]{2,1,0:T(8,128)}) %reduce-scatter.31.cloned.1.call-update) | async-done | bytes 1060880
  1090.4 1.3 convert_bitcast_fusion.5
  1091.7 1.1 add_bitcast_fusion.2
  1092.7 178.8 %reduce-scatter.37.cloned.1.call-done = f32[1,56,4736]{2,1,0:T(8,128)} async-done(((f32[1,896,4736]{2,1,0:T(8,128)}), f32[1,56,4736]{2,1,0:T(8,128)}) %reduce-scatter.37.cloned.1.call-update) | async-done | bytes 1060880
  1271.5 1.3 convert_bitcast_fusion.2
  1272.8 180.0 %reduce-scatter.35.cloned.1.call-done = f32[1,56,4736]{2,1,0:T(8,128)} async-done(((f32[1,896,4736]{2,1,0:T(8,128)}), f32[1,56,4736]{2,1,0:T(8,128)}) %reduce-scatter.35.cloned.1.call-update) | async-done | bytes 1060880
  1452.8 1.3 convert_bitcast_fusion.3
  1454.1 1.1 add_bitcast_fusion.1
  1455.2 178.8 %reduce-scatter.39.cloned.1.call-done = f32[1,296,896]{2,1,0:T(8,128)} async-done(((f32[1,4736,896]{2,1,0:T(8,128)}), f32[1,296,896]{2,1,0:T(8,128)}) %reduce-scatter.39.cloned.1.call-update) | async-done | bytes 1060880
  1634.0 1.3 convert_bitcast_fusion.1
  1635.2 1.1 add_bitcast_fusion
  (57 shorter events, 0.6 us)
Async XLA Ops:
  7.2 9.0 copy-start.3
  7.2 81.6 %all-gather.32.cloned.1.call-start = ((), (), s32[]{:S(2)}) async-start(), calls=%async_computation.7 | async-start | bytes 9017344 | tf_op jit(solution)/vmap(jvp())/squeeze | solution.py:27
  9.6 154.7 %all-gather.30.cloned.1.call-start = ((), (), s32[]{:S(2)}) async-start(), calls=%async_computation.6 | async-start | bytes 9017344 | tf_op jit(solution)/vmap(jvp())/squeeze | solution.py:27
  11.9 228.0 %all-gather.34.cloned.1.call-start = ((), (), s32[]{:S(2)}) async-start(), calls=%async_computation.8 | async-start | bytes 9017344 | tf_op jit(solution)/vmap(jvp())/squeeze | solution.py:27
  14.3 301.1 %all-gather.38.cloned.1.call-start = ((), (), s32[]{:S(2)}) async-start(), calls=%async_computation.10 | async-start | bytes 9017344 | tf_op jit(solution)/vmap(jvp())/squeeze | solution.py:27
  14.9 376.6 %all-gather.36.cloned.1.call-start = ((), (), s32[]{:S(2)}) async-start(), calls=%async_computation.9 | async-start | bytes 9017344 | tf_op jit(solution)/vmap(jvp())/squeeze | solution.py:27
  15.5 452.0 %all-gather.40.cloned.1.call-start = ((), (), s32[]{:S(2)}) async-start(), calls=%async_computation.11 | async-start | bytes 9017344 | tf_op jit(solution)/vmap(jvp())/squeeze | solution.py:27
  16.1 711.7 %reduce-scatter.41.cloned.1.call-start = ((), (), s32[]{:S(2)}) async-start(), calls=%async_computation.17 | async-start | bytes 18034688
  177.9 6.5 copy-start
  184.4 55.6 %copy-start.4 = (bf16[1,1024,896]{1,2,0:T(8,128)(2,1)S(1)}, bf16[1,1024,896]{1,2,0:T(8,128)(2,1)}, u32[]{:S(2)}) copy-start(bf16[1,1024,896]{1,2,0:T(8,128)(2,1)} %copy.1) | copy-start | bytes 5505028
  255.6 135.9 %copy-start.9 = (bf16[1,1,1024,896]{2,3,1,0:T(8,128)(2,1)S(1)}, bf16[1,1,1024,896]{2,3,1,0:T(8,128)(2,1)}, u32[]{:S(2)}) copy-start(bf16[1,1,1024,896]{2,3,1,0:T(8,128)(2,1)} %get-tuple-element.15) | copy-start | bytes 5505028
  467.5 17.3 %copy-start.1 = (f32[1024,4736]{1,0:T(8,128)S(1)}, f32[1024,4736]{1,0:T(8,128)}, u32[]{:S(2)}) copy-start(f32[1024,4736]{1,0:T(8,128)} %fusion.43) | copy-start | bytes 58195972
  502.0 36.4 %slice-start.3 = ((s8[9699328]{0:T(1024)(128)(4,1)}), s8[1310720]{0:T(1024)(128)(4,1)S(1)}, s32[]{:S(2)}) async-start(s8[9699328]{0:T(1024)(128)(4,1)} %bitcast.257), calls=%async_computation.21 | async-start | bytes 2621440
  502.0 36.4 %slice-start.4 = ((s8[9699328]{0:T(1024)(128)(4,1)}), s8[4194304]{0:T(1024)(128)(4,1)S(1)}, s32[]{:S(2)}) async-start(s8[9699328]{0:T(1024)(128)(4,1)} %bitcast.257), calls=%async_computation.22 | async-start | bytes 8388608
  520.3 15.5 copy-start.7
  520.3 15.5 copy-start.10
  520.3 18.1 %slice-start.5 = ((s8[9699328]{0:T(1024)(128)(4,1)}), s8[4194304]{0:T(1024)(128)(4,1)S(1)}, s32[]{:S(2)}) async-start(s8[9699328]{0:T(1024)(128)(4,1)} %bitcast.257), calls=%async_computation.23 | async-start | bytes 8388608
  537.1 1.2 copy-start.8
  551.4 357.7 %reduce-scatter.33.cloned.1.call-start = ((), (), s32[]{:S(2)}) async-start(), calls=%async_computation.13 | async-start | bytes 18034688
  566.1 3.7 copy-start.2
  588.7 35.5 %slice-start = ((s8[9699328]{0:T(1024)(128)(4,1)}), s8[1310720]{0:T(1024)(128)(4,1)S(1)}, s32[]{:S(2)}) async-start(s8[9699328]{0:T(1024)(128)(4,1)} %bitcast.255), calls=%async_computation.18 | async-start | bytes 2621440
  588.8 35.5 %slice-start.1 = ((s8[9699328]{0:T(1024)(128)(4,1)}), s8[4194304]{0:T(1024)(128)(4,1)S(1)}, s32[]{:S(2)}) async-start(s8[9699328]{0:T(1024)(128)(4,1)} %bitcast.255), calls=%async_computation.19 | async-start | bytes 8388608
  607.1 16.6 %copy-start.13 = (f32[1024]{0:T(1024)S(1)}, f32[1024]{0:T(1024)}, u32[]{:S(2)}) copy-start(f32[1024]{0:T(1024)} %get-tuple-element.12) | copy-start | bytes 12292
  607.1 17.2 %slice-start.2 = ((s8[9699328]{0:T(1024)(128)(4,1)}), s8[4194304]{0:T(1024)(128)(4,1)S(1)}, s32[]{:S(2)}) async-start(s8[9699328]{0:T(1024)(128)(4,1)} %bitcast.255), calls=%async_computation.20 | async-start | bytes 8388608
  607.1 17.2 %copy-start.5 = (bf16[1,1024,896]{1,2,0:T(8,128)(2,1)S(1)}, bf16[1,1024,896]{1,2,0:T(8,128)(2,1)}, u32[]{:S(2)}) copy-start(bf16[1,1024,896]{1,2,0:T(8,128)(2,1)} %copy.1) | copy-start | bytes 5505028
  636.2 1.5 copy-start.11
  636.2 454.2 %reduce-scatter.31.cloned.1.call-start = ((), (), s32[]{:S(2)}) async-start(), calls=%async_computation.12 | async-start | bytes 18034688
  653.2 1.5 copy-start.6
  653.2 618.3 %reduce-scatter.37.cloned.1.call-start = ((), (), s32[]{:S(2)}) async-start(), calls=%async_computation.15 | async-start | bytes 18034688
  673.4 779.4 %reduce-scatter.35.cloned.1.call-start = ((), (), s32[]{:S(2)}) async-start(), calls=%async_computation.14 | async-start | bytes 18034688
  693.0 940.9 %reduce-scatter.39.cloned.1.call-start = ((), (), s32[]{:S(2)}) async-start(), calls=%async_computation.16 | async-start | bytes 18034688
  717.3 0.7 copy-start.12
Sparse Core Ops, SparseCore 0:
  10.8 77.8 all-gather.31
  91.0 73.3 all-gather.29
  166.6 73.3 all-gather.33
  242.1 73.3 all-gather.37
  318.1 73.3 all-gather.35
  394.2 73.3 all-gather.39
  551.5 176.2 reduce-scatter.40
  731.8 177.2 reduce-scatter.32
  913.1 177.2 reduce-scatter.30
  1094.2 177.2 reduce-scatter.36
  1275.5 177.2 reduce-scatter.34
  1456.7 177.2 reduce-scatter.38
where the time goes:
time: 1660 us; the launch traced here: 1640 us
  waiting for transfers between devices  1240 us (75%)
  matrix products  283 us (17%)
  other arithmetic  68.6 us (4%)
  local copies, waits for them, and re-layouts  31.9 us (2%)
    unnamed x18, waiting for transfers between devices  901 us
    squeeze x6, waiting for transfers between devices, stack(): h = layer(h, {name: w[number] for name, w in weights.items()})  344 us
    dot_general x6, matrix products, layer(): up = jnp.dot(a, w['w_up'], preferred_element_type=jnp.float32)  110 us
    dot_general x6, matrix products, layer(): gate = jnp.dot(a, w['w_gate'], preferred_element_type=jnp.float32)  89.6 us
    dot_general x5, matrix products, matmul(): jnp.dot(a, w, preferred_element_type=jnp.float32).astype(jnp.bfloat16)  84.1 us
    unnamed x5, other arithmetic  50 us
  transfers between devices with their start and end apart: 12, of which 12 were waited for; matrix products, arithmetic and copies ran while one was open for 17% of the time, Pallas kernels for 0%

commit v1 on v0

v1 whole, which is shorter than its diff:
```python
import functools

import jax
import jax.numpy as jnp
from jax import lax
from jax.experimental import pallas as pl
from jax.experimental.pallas import tpu as pltpu
from jax.sharding import PartitionSpec as P

MESH = pl.DeviceIdType.MESH
BF16, F32 = jnp.bfloat16, jnp.float32
LAYERS, T, D, FF = 2, 1024, 896, 4736
N = 16
TILE = 256
TILES = 19
FFP = TILE * TILES
RG, RD = D // N, FF // N
EPS = 1e-6
CH = 128
ROW_CHUNKS = 2
ROWS = T // ROW_CHUNKS

GU_B, GU_A = 1664, 1536
D_B, D_A = 104, 96
D_SUBS_B, D_SUBS_A = ((0, 56), (56, 48)), ((0, 48), (48, 48))


class Place:
    def __init__(self):
        self.rep = lax.axis_index("rep")
        me = lax.axis_index("dp")
        self.core = lax.rem(me, 2)
        self.chip = me // 2
        self.ring = jnp.where(self.chip < 4, self.chip, 11 - self.chip)
        self.way = 1 - 2 * self.core
        self.next = (self.rep, self.device(1))
        self.prev = (self.rep, self.device(-1))
        self.sibling = (self.rep, self.chip * 2 + 1 - self.core)
        self.other = (1 - self.rep, me)

    def chip_at(self, steps):
        r = lax.rem(self.ring + self.way * steps + 16, 8)
        return jnp.where(r < 4, r, 11 - r)

    def device(self, steps):
        return self.chip_at(steps) * 2 + self.core


def barrier(devices):
    sem = pltpu.get_barrier_semaphore()
    for device in devices:
        pl.semaphore_signal(sem, inc=1, device_id=device, device_id_type=MESH)
    pl.semaphore_wait(sem, len(devices))


def remote(src, dst, send, recv, device):
    return pltpu.make_async_remote_copy(
        src_ref=src, dst_ref=dst, send_sem=send, recv_sem=recv, device_id=device, device_id_type=MESH
    )


def loop(lo, hi, body):
    def run(i, carry):
        body(i)
        return carry

    lax.fori_loop(lo, hi, run, 0)


def start(copies):
    for copy in copies:
        copy.start()


def wait(copies):
    for copy in copies:
        copy.wait()


def mult(x, m):
    return pl.multiple_of(x, m)


def dot(a, b, dims=((1,), (0,))):
    return lax.dot_general(a, b, (dims, ((), ())), preferred_element_type=F32)


def forward_kernel(
    x_ref, wg_ref, wu_ref, wd_ref,
    g_out, d_out, p_out, q_out, actt_out, at_out, h1_out,
    a_s, h_s, hacc, wgu_t, wd_t, p_s, q_s, pt_s, at_s, zc, zr,
    ring_recv, x_recv, sib_recv, ring_send, x_send, sib_send, local_sem, w_sem, o_sem, at_sem,
):
    here = Place()
    barrier((here.next, here.prev, here.sibling, here.other))

    def gu_part(ref, dev, a_group):
        rows = pl.ds(mult(dev * RG, 8), RG)
        if a_group is None:
            return ref.at[rows, pl.ds(0, GU_B)]
        return ref.at[rows, pl.ds(mult(GU_B + GU_A * a_group, 128), GU_A)]

    def d_part(ref, dev, a_group, sub):
        if a_group is None:
            start, size = D_SUBS_B[sub]
        else:
            start, size = D_SUBS_A[sub]
            start = D_B + D_A * a_group + start
        return ref.at[pl.ds(mult(dev * RD + start, 8), size), :]

    GU_ITEMS = ((0, False, 0, 0), (1, False, 0, 0), (0, True, 0, 1), (1, True, 0, 1))
    D_ITEMS = ((2, False, 0, 0), (2, True, 0, 2), (2, False, 1, 1), (2, True, 1, 3))

    def region(l, item, dev, group):
        mat, own, sub, _ = item
        if mat < 2:
            return gu_part(g_out.at[l, mat], dev, group if own else None)
        return d_part(d_out.at[l], dev, group if own else None, sub)

    def rr(l, mat, t, slot):
        return ring_recv.at[((l * 3 + mat) * 7 + t - 1) * 4 + slot]

    def xr(l, mat, t, sub):
        return x_recv.at[((l * 3 + mat) * 7 + t - 1) * 2 + sub]

    def lm(l, mat):
        return l * 3 + mat

    def to_sibling(l, mat, src, dst):
        remote(src, dst, sib_send.at[lm(l, mat)], sib_recv.at[lm(l, mat)], here.sibling).start()

    def ring_event(l, t, item):
        mat, own, sub, slot = item
        reg = region(l, item, here.device(-t), here.rep)
        remote(reg, reg, ring_send.at[lm(l, mat)], rr(l, mat, t, slot), here.next).wait_recv()

        @pl.when(t < 7)
        def _():
            remote(reg, reg, ring_send.at[lm(l, mat)], rr(l, mat, t + 1, slot), here.next).start()

        if own:
            remote(reg, reg, x_send.at[lm(l, mat)], xr(l, mat, t, sub), here.other).start()
        to_sibling(l, mat, reg, reg)

    def x_event(l, t, item):
        mat, _, sub, _ = item
        reg = region(l, item, here.device(-t), 1 - here.rep)
        remote(reg, reg, x_send.at[lm(l, mat)], xr(l, mat, t, sub), here.other).wait_recv()
        to_sibling(l, mat, reg, reg)

    def x_events(l, t, items):
        for item in items:
            if item[1]:
                x_event(l, t, item)

    def start_own(l, mats):
        me = here.device(0)
        for mat in mats:
            src = (wg_ref, wu_ref, wd_ref)[mat].at[l]
            items = [i for i in GU_ITEMS + D_ITEMS if i[0] == mat]
            for item in items:
                _, own, sub, slot = item
                group = here.rep if own else None
                part = gu_part(src, 0, group) if mat < 2 else d_part(src, 0, group, sub)
                remote(
                    part, region(l, item, me, here.rep), ring_send.at[lm(l, mat)], rr(l, mat, 1, slot), here.next
                ).start()
        for mat in mats:
            src = (wg_ref, wu_ref, wd_ref)[mat].at[l]
            if mat < 2:
                whole = g_out.at[l, mat, pl.ds(mult(me * RG, 8), RG), pl.ds(0, FF)]
            else:
                whole = d_out.at[l, pl.ds(mult(me * RD, 8), RD), :]
            to_sibling(l, mat, src, whole)
            pltpu.make_async_copy(src, whole, local_sem.at[lm(l, mat)]).start()

    def wait_own(l, mats):
        for mat in mats:
            src = (wg_ref, wu_ref, wd_ref)[mat].at[l]
            pltpu.make_async_copy(src, src, local_sem.at[lm(l, mat)]).wait()

    def wait_sibling(l, mat):
        half = g_out.at[l, mat, pl.ds(0, D // 2), pl.ds(0, FF)] if mat < 2 else d_out.at[l, pl.ds(0, FF // 2), :]
        remote(half, half, sib_send.at[lm(l, mat)], sib_recv.at[lm(l, mat)], here.sibling).wait_recv()

    def wait_sends(l):
        for mat in range(3):
            if mat < 2:
                rows = pl.ds(0, 7 * RG)
                sent = [g_out.at[l, mat, rows, pl.ds(0, GU_B + GU_A)], g_out.at[l, mat, rows, pl.ds(0, GU_A)]]
                half = g_out.at[l, mat, pl.ds(0, D // 2), pl.ds(0, FF)]
            else:
                sent = [d_out.at[l, pl.ds(0, 7 * (D_B + D_A)), :], d_out.at[l, pl.ds(0, 7 * D_A), :]]
                half = d_out.at[l, pl.ds(0, FF // 2), :]
            for ref, sem in zip(sent + [half], (ring_send, x_send, sib_send)):
                remote(ref, ref, sem.at[lm(l, mat)], sem.at[lm(l, mat)], here.next).wait_send()

    start_own(0, (0, 1, 2))

    zc[...] = jnp.zeros_like(zc)
    zr[...] = jnp.zeros_like(zr)
    pads = [(zc, g_out.at[l, m, :, pl.ds(FF, FFP - FF)]) for l in range(LAYERS) for m in range(2)]
    pads += [(zr, d_out.at[l, pl.ds(FF, FFP - FF), :]) for l in range(LAYERS)]
    for i, (src, dst) in enumerate(pads):
        pltpu.make_async_copy(src, dst, local_sem.at[6 + i]).start()

    def norm(src):
        def chunk(i):
            rows = pl.ds(mult(i * CH, CH), CH)
            wide = src[rows, :].astype(F32)
            a = wide * lax.rsqrt(jnp.mean(wide * wide, -1, keepdims=True) + EPS)
            a_s[rows, :] = a.astype(BF16)
            at_s[:, rows] = a.astype(BF16).T

        loop(0, T // CH, chunk)

    def put_at(l):
        return pltpu.make_async_copy(at_s, at_out.at[l], at_sem)

    norm(x_ref)
    put_at(0).start()

    def first(t):
        for item in GU_ITEMS + D_ITEMS:
            ring_event(0, t, item)

        @pl.when(t == 6)
        def _():
            start_own(1, (0, 1))

        @pl.when(t > 1)
        def _():
            x_events(0, t - 1, GU_ITEMS + D_ITEMS)

    loop(1, 8, first)
    x_events(0, 7, GU_ITEMS + D_ITEMS)
    for i, (src, dst) in enumerate(pads):
        pltpu.make_async_copy(src, dst, local_sem.at[6 + i]).wait()
    wait_own(0, (0, 1, 2))
    for mat in range(3):
        wait_sibling(0, mat)

    def layer(l, items, after_six):
        with_h = l == 0

        def loads(j, slot):
            cols = pl.ds(mult(j * TILE, TILE), TILE)
            pairs = [(g_out.at[l, m, :, cols], wgu_t.at[slot, :, pl.ds(m * TILE, TILE)]) for m in range(2)]
            if with_h:
                pairs.append((d_out.at[l, cols, :], wd_t.at[slot]))
            return [pltpu.make_async_copy(src, dst, w_sem.at[slot, i]) for i, (src, dst) in enumerate(pairs)]

        def stores(j, slot):
            rows = pl.ds(mult(j * TILE, TILE), TILE)
            pairs = ((p_s, p_out.at[l, j]), (q_s, q_out.at[l, j]), (pt_s, actt_out.at[l, rows, :]))
            return [pltpu.make_async_copy(src.at[slot], dst, o_sem.at[slot, i]) for i, (src, dst) in enumerate(pairs)]

        start(loads(0, 0))

        def tick(j):
            slot = lax.rem(j, 2)

            @pl.when(j + 1 < TILES)
            def _():
                start(loads(j + 1, 1 - slot))

            wait(loads(j, slot))

            @pl.when(j >= 2)
            def _():
                wait(stores(j - 2, slot))

            for r in range(ROW_CHUNKS):
                rows = pl.ds(r * ROWS, ROWS)
                both = dot(a_s[rows, :], wgu_t[slot])
                gate, up = both[:, :TILE], both[:, TILE:]
                s = 0.5 * jnp.tanh(0.5 * gate) + 0.5
                q = gate * s
                q_s[slot, rows, :] = q
                p_s[slot, rows, :] = up * (s + q * (1 - s))
                prod = (q * up).astype(BF16)
                pt_s[slot, :, rows] = prod.T
                if with_h:
                    hacc[rows, :] += dot(prod, wd_t[slot])
            start(stores(j, slot))

            def event(e):
                t = e // 4 + 1
                for i, item in enumerate(items):
                    pl.when(lax.rem(e, 4) == i)(functools.partial(ring_event, 1, t, item))
                pl.when(e == 4 * 6 - 1)(after_six)
                pl.when((lax.rem(e, 4) == 3) & (t > 1))(functools.partial(x_events, 1, t - 1, items))

            loop((j * 28) // TILES, ((j + 1) * 28) // TILES, event)

        loop(0, TILES, tick)
        x_events(1, 7, items)
        for j in (TILES - 2, TILES - 1):
            wait(stores(j, j % 2))

    hacc[...] = jnp.zeros_like(hacc)
    layer(0, GU_ITEMS, lambda: start_own(1, (2,)))

    def new_h(i):
        rows = pl.ds(mult(i * CH, CH), CH)
        y = hacc[rows, :].astype(BF16)
        h_s[rows, :] = (x_ref[rows, :].astype(F32) + y.astype(F32)).astype(BF16)

    loop(0, T // CH, new_h)
    put_h = pltpu.make_async_copy(h_s, h1_out, at_sem)
    put_at(0).wait()
    norm(h_s)
    put_h.start()
    put_h.wait()
    put_at(1).start()
    wait_own(1, (0, 1))
    wait_sibling(1, 0)
    wait_sibling(1, 1)
    layer(1, D_ITEMS, lambda: None)
    wait_own(1, (2,))
    wait_sibling(1, 2)
    put_at(1).wait()
    for l in range(LAYERS):
        wait_sends(l)


def forward(x, wg, wu, wd):
    any_, vmem = pl.BlockSpec(memory_space=pl.ANY), pl.BlockSpec(memory_space=pltpu.VMEM)
    dma = pltpu.SemaphoreType.DMA
    return pl.pallas_call(
        forward_kernel,
        out_shape=(
            jax.ShapeDtypeStruct((LAYERS, 2, D, FFP), BF16),
            jax.ShapeDtypeStruct((LAYERS, FFP, D), BF16),
            jax.ShapeDtypeStruct((LAYERS, TILES, T, TILE), F32),
            jax.ShapeDtypeStruct((LAYERS, TILES, T, TILE), F32),
            jax.ShapeDtypeStruct((LAYERS, FFP, T), BF16),
            jax.ShapeDtypeStruct((LAYERS, D, T), BF16),
            jax.ShapeDtypeStruct((T, D), BF16),
        ),
        in_specs=[vmem] * 4,
        out_specs=(any_,) * 7,
        scratch_shapes=[
            pltpu.VMEM((T, D), BF16),
            pltpu.VMEM((T, D), BF16),
            pltpu.VMEM((T, D), F32),
            pltpu.VMEM((2, D, 2 * TILE), BF16),
            pltpu.VMEM((2, TILE, D), BF16),
            pltpu.VMEM((2, T, TILE), F32),
            pltpu.VMEM((2, T, TILE), F32),
            pltpu.VMEM((2, TILE, T), BF16),
            pltpu.VMEM((D, T), BF16),
            pltpu.VMEM((D, FFP - FF), BF16),
            pltpu.VMEM((FFP - FF, D), BF16),
            dma((2 * 3 * 7 * 4,)),
            dma((2 * 3 * 7 * 2,)),
            dma((6,)),
            dma((6,)),
            dma((6,)),
            dma((6,)),
            dma((12,)),
            dma((2, 3)),
            dma((2, 3)),
            dma(()),
        ],
        compiler_params=pltpu.CompilerParams(
            collective_id=0, has_side_effects=True, vmem_limit_bytes=56 * 1024 * 1024
        ),
        name="forward_gather",
    )(x, wg, wu, wd)


PAIRS, STEPS, PLACES = 6, 8, 4
PER_PAIR = STEPS // 2 * PLACES
D_PART, C_PART = 72, 5 * TILE
D_LAST, C_LAST = RD - 3 * D_PART, FF - 3 * C_PART
D_PAIRS = 2
LAST_EVENT = (LAYERS * PAIRS + 1) * PER_PAIR
AHEAD = PLACES - 1
LAG = 2 * PLACES
FIRST_EVENT = 2
PAIR_EVENTS, TILE_EVENTS = 12, 54


def backward_kernel(
    dy_ref, x_ref, h1_ref, g_ref, d_ref, p_ref, q_ref, actt_ref, at_ref,
    dx_out, dgu_out, dd_out, own_gu, sib_gu, own_d, sib_d,
    dh_s, at_s, h_s, dacc, lhs_t, blk_s, wgu_t, wd_t, p_t, q_t, dz_s, term_s, slot_d, slot_c, st_d, st_c,
    ring_recv, ring_send, st_sem, fin_sem, sd_recv, sgu_recv, lhs_sem, blk_sem, blk_send, w_sem, term_sem, term_send, misc_sem,
):
    here = Place()
    barrier((here.next, here.prev, here.sibling))

    def chips(s):
        return here.chip_at(-1 - s), here.chip_at(1 + s)

    class Lane:
        def __init__(self, l, pair, lane, s, place, down, last):
            chip, _ = chips(s)
            self.s, self.place = s, place
            self.sems = [sem.at[l, pair, lane] for sem in (ring_recv, ring_send)]
            self.fin = fin_sem.at[l, pair, lane]
            if down:
                part = pair * 2 + lane
                rows, cut = (pl.ds(first, D_LAST if last else D_PART) for first in (mult(part * D_PART, 8), 0))
                self.slots = [slot_d.at[pair, lane, to, cut, :] for to in (s, s + 1)]
                self.st = [st_d.at[place, i, cut, :] for i in range(2)]
                self.terms = [ref.at[l, chip, rows, :] for ref in (own_d, sib_d)]
                self.result = dd_out.at[l, rows, :]
            else:
                part = pair - D_PAIRS
                cols, cut = (pl.ds(first, C_LAST if last else C_PART) for first in (mult(part * C_PART, 128), 0))
                self.slots = [slot_c.at[part, lane, to, :, cut] for to in (s, s + 1)]
                self.st = [st_c.at[place, i, :, cut] for i in range(2)]
                self.terms = [ref.at[l, lane, chip, :, cols] for ref in (own_gu, sib_gu)]
                self.result = dgu_out.at[lane, l, :, cols]

        def stage(self):
            pairs = zip(self.terms, self.st)
            return [pltpu.make_async_copy(a, b, st_sem.at[self.place, i]) for i, (a, b) in enumerate(pairs)]

        def send(self, to):
            recv, sent = self.sems
            return remote(self.slots[0], self.slots[to], sent.at[self.s], recv.at[self.s + to], here.next)

        def finish(self):
            return pltpu.make_async_copy(self.slots[0], self.result, self.fin)

        def step(self):
            wait(self.stage())
            slot = self.slots[0]
            ends = [st[...].astype(F32) for st in self.st]

            @pl.when(self.s > 0)
            def _():
                self.send(0).wait_recv()
                slot[...] = (slot[...].astype(F32) + (ends[0] + ends[1])).astype(BF16)

            @pl.when(self.s == 0)
            def _():
                slot[...] = (ends[0] + ends[1]).astype(BF16)

            pl.when(self.s < STEPS - 1)(lambda: self.send(1).start())
            pl.when(self.s == STEPS - 1)(lambda: self.finish().start())

        def wait_out(self):
            pl.when(self.s < STEPS - 1)(lambda: self.send(1).wait_send())
            pl.when(self.s == STEPS - 1)(lambda: self.finish().wait())

        def prefetch(self):
            start(self.stage())

    def with_lane(e, action, ahead_of=lambda l, pair, lane, s: None):
        round_, place = e // PLACES, lax.rem(e, PLACES)
        new = place // 2
        index = round_ // PLACES + new - 1
        s = lax.rem(round_, PLACES) + PLACES * (1 - new)
        lane = lax.rem(place, 2)

        @pl.when((index >= 0) & (index < LAYERS * PAIRS))
        def _():
            behind = jnp.where(index < PAIRS, 0, 1)
            l, pair = 1 - behind, index - PAIRS * behind
            ahead_of(l, pair, lane, s)
            down = pair < D_PAIRS
            last_d = (pair == D_PAIRS - 1) & (lane == 1)
            last_c = pair == PAIRS - 1
            for is_down, is_last, chosen in (
                (True, False, down & ~last_d), (True, True, last_d),
                (False, False, ~down & ~last_c), (False, True, last_c),
            ):
                pl.when(chosen)(lambda: action(Lane(l, pair, lane, s, place, is_down, is_last)))

    def terms_ready(l, pair, lane, s):
        @pl.when((pair == 0) & (lane == 0))
        def _():
            whole = sib_d.at[l, 0]
            remote(whole, whole, blk_send.at[0], sd_recv.at[l, s], here.sibling).wait_recv()

        @pl.when((pair >= D_PAIRS) & (lane == 0) & (s == 0))
        def _():
            for is_last in (False, True):
                width = FFP - 3 * C_PART if is_last else C_PART

                @pl.when((pair == PAIRS - 1) == is_last)
                def _(width=width):
                    part = sib_gu.at[l, :, :, :, pl.ds(0, width)]
                    sem = sgu_recv.at[l, pair - D_PAIRS]
                    remote(part, part, term_send.at[0, 0], sem, here.sibling).wait_recv()

    def fetch(e):
        with_lane(e, Lane.prefetch, terms_ready)

    def event(e):
        pl.when(e >= LAG)(lambda: with_lane(e - LAG, Lane.wait_out))
        fetch(e + AHEAD)
        with_lane(e, Lane.step)

    def lhs_loads(l, s, slot):
        mine, other = chips(s)
        rows = ((mine * 2 + here.core) * RD, (other * 2 + 1 - here.core) * RD)
        return [
            pltpu.make_async_copy(actt_ref.at[l, pl.ds(mult(row, 8), RD), :], lhs_t.at[slot, i], lhs_sem.at[slot, i])
            for i, row in enumerate(rows)
        ]

    def block_copies(l, s, slot):
        mine, other = chips(s)
        return (
            pltpu.make_async_copy(blk_s.at[slot, 0], own_d.at[l, mine], blk_sem.at[slot]),
            remote(blk_s.at[slot, 1], sib_d.at[l, other], blk_send.at[slot], sd_recv.at[l, s], here.sibling),
        )

    def tile_loads(l, j, slot):
        cols = pl.ds(mult(j * TILE, TILE), TILE)
        pairs = [(d_ref.at[l, cols, :], wd_t.at[slot]), (p_ref.at[l, j], p_t.at[slot]), (q_ref.at[l, j], q_t.at[slot])]
        pairs += [(g_ref.at[l, m, :, cols], wgu_t.at[slot, :, pl.ds(m * TILE, TILE)]) for m in range(2)]
        return [pltpu.make_async_copy(src, dst, w_sem.at[slot, i]) for i, (src, dst) in enumerate(pairs)]

    def term_copies(l, j, slot):
        cols = pl.ds(mult(j * TILE, TILE), TILE)
        part = jnp.minimum(j // (C_PART // TILE), PAIRS - D_PAIRS - 1)
        own, sib = [], []
        for m in range(2):
            mine, other = term_s.at[slot, m, :, here.core], term_s.at[slot, m, :, 1 - here.core]
            own.append(pltpu.make_async_copy(mine, own_gu.at[l, m, :, :, cols], term_sem.at[slot, m]))
            to = sib_gu.at[l, m, :, :, cols]
            sib.append(remote(other, to, term_send.at[slot, m], sgu_recv.at[l, part], here.sibling))
        return own, sib

    def wait_terms(l, j, slot):
        own, sib = term_copies(l, j, slot)
        wait(own)
        for copy in sib:
            copy.wait_send()

    def wait_block(l, s, slot):
        own, sib = block_copies(l, s, slot)
        own.wait()
        sib.wait_send()

    def layer(i):
        l = 1 - i
        base = FIRST_EVENT + i * (PAIR_EVENTS + TILE_EVENTS)
        load_at = pltpu.make_async_copy(at_ref.at[l], at_s, misc_sem.at[0])
        load_at.start()
        pl.when(i == 0)(pltpu.make_async_copy(h1_ref, h_s, misc_sem.at[1]).start)
        pl.when(i == 1)(pltpu.make_async_copy(x_ref, h_s, misc_sem.at[1]).start)
        start(lhs_loads(l, 0, 0))
        start(tile_loads(l, 0, 0))

        def pair(s):
            slot = lax.rem(s, 2)
            pl.when(s < STEPS - 1)(lambda: start(lhs_loads(l, s + 1, 1 - slot)))
            wait(lhs_loads(l, s, slot))
            for b in range(2):
                blk_s[slot, b] = dot(lhs_t[slot, b], dh_s[...]).astype(BF16)
            start(block_copies(l, s, slot))
            pl.when(s >= 1)(lambda: wait_block(l, s - 1, 1 - slot))
            pl.when((i == 0) & (s == 1))(lambda: loop(FIRST_EVENT, FIRST_EVENT + AHEAD, fetch))

            def done_by(s):
                cap = jnp.where(i == 0, jnp.maximum(PLACES * s - 1, FIRST_EVENT), LAST_EVENT)
                return jnp.minimum(base + (PAIR_EVENTS * (s + 1)) // STEPS, cap)

            loop(jnp.where(s == 0, base, done_by(s - 1)), done_by(s), event)

        loop(0, STEPS, pair)
        wait_block(l, STEPS - 1, (STEPS - 1) % 2)
        load_at.wait()
        dacc[...] = jnp.zeros_like(dacc)

        def tick(j):
            slot = lax.rem(j, 2)
            pl.when(j + 1 < TILES)(lambda: start(tile_loads(l, j + 1, 1 - slot)))
            wait(tile_loads(l, j, slot))
            pl.when(j >= 2)(lambda: wait_terms(l, j - 2, slot))

            def done_by(j, half):
                cap = jnp.where(i == 0, PER_PAIR * (D_PAIRS + (j + 4) // (C_PART // TILE) - 1) - 1, LAST_EVENT)
                return jnp.minimum(base + PAIR_EVENTS + ((2 * j + half) * TILE_EVENTS) // (2 * TILES), cap)

            for r in range(ROW_CHUNKS):
                rows = pl.ds(r * ROWS, ROWS)
                dprod = dot(dh_s[rows, :], wd_t[slot], ((1,), (1,))).astype(BF16).astype(F32)
                dz_s[rows, pl.ds(0, TILE)] = (dprod * p_t[slot, rows, :]).astype(BF16)
                dz_s[rows, pl.ds(TILE, TILE)] = (dprod * q_t[slot, rows, :]).astype(BF16)
                dacc[rows, :] += dot(dz_s[rows, :], wgu_t[slot], ((1,), (1,)))
            loop(jnp.where(j == 0, base + PAIR_EVENTS, done_by(j - 1, 2)), done_by(j, 1), event)
            for r in range(2):
                term = dot(at_s[pl.ds(r * D // 2, D // 2), :], dz_s[...])
                for b in range(8):
                    for m in range(2):
                        block = term[b * RG : (b + 1) * RG, m * TILE : (m + 1) * TILE]
                        term_s[slot, m, r * 4 + b // 2, b % 2] = block.astype(BF16)
            own, sib = term_copies(l, j, slot)
            start(own + sib)
            loop(done_by(j, 1), done_by(j, 2), event)

        loop(0, TILES, tick)
        for j in (TILES - 2, TILES - 1):
            wait_terms(l, j, j % 2)
        pltpu.make_async_copy(h1_ref, h_s, misc_sem.at[1]).wait()

        def new_dh(r):
            rows = pl.ds(mult(r * CH, CH), CH)
            da = dacc[rows, :].astype(BF16).astype(F32)
            wide = h_s[rows, :].astype(F32)
            scale = lax.rsqrt(jnp.mean(wide * wide, -1, keepdims=True) + EPS)
            along = jnp.mean(da * wide, -1, keepdims=True) * scale * scale
            by_h = (scale * (da - wide * along)).astype(BF16).astype(F32)
            dh_s[rows, :] = (dh_s[rows, :].astype(F32) + by_h).astype(BF16)

        loop(0, T // CH, new_dh)

    load_dy = pltpu.make_async_copy(dy_ref, dh_s, misc_sem.at[2])
    load_dy.start()
    load_dy.wait()
    loop(0, LAYERS, layer)
    put_dx = pltpu.make_async_copy(dh_s, dx_out, misc_sem.at[2])
    put_dx.start()
    loop(FIRST_EVENT + LAYERS * (PAIR_EVENTS + TILE_EVENTS), LAST_EVENT, event)
    loop(LAST_EVENT - LAG, LAST_EVENT, lambda e: with_lane(e, Lane.wait_out))
    put_dx.wait()


def backward(dy, x, h1, gathered_gu, gathered_d, p, q, actt, at):
    any_ = pl.BlockSpec(memory_space=pl.ANY)
    vmem, dma = pltpu.VMEM, pltpu.SemaphoreType.DMA
    terms_gu = jax.ShapeDtypeStruct((LAYERS, 2, 8, RG, FFP), BF16)
    terms_d = jax.ShapeDtypeStruct((LAYERS, 8, RD, D), BF16)
    two = (2, 2)
    per_part = (LAYERS, PAIRS, 2)
    outs = (
        jax.ShapeDtypeStruct((T, D), BF16),
        jax.ShapeDtypeStruct((2, LAYERS, RG, FF), BF16),
        jax.ShapeDtypeStruct((LAYERS, RD, D), BF16),
        terms_gu, terms_gu, terms_d, terms_d,
    )
    return pl.pallas_call(
        backward_kernel,
        out_shape=outs,
        in_specs=[any_] * 9,
        out_specs=(any_,) * len(outs),
        scratch_shapes=[
            vmem((T, D), BF16),
            vmem((D, T), BF16),
            vmem((T, D), BF16),
            vmem((T, D), F32),
            vmem((*two, RD, T), BF16),
            vmem((*two, RD, D), BF16),
            vmem((2, D, 2 * TILE), BF16),
            vmem((2, TILE, D), BF16),
            vmem((2, T, TILE), F32),
            vmem((2, T, TILE), F32),
            vmem((T, 2 * TILE), BF16),
            vmem((*two, 8, 2, RG, TILE), BF16),
            vmem((D_PAIRS, 2, STEPS, D_LAST, D), BF16),
            vmem((PAIRS - D_PAIRS, 2, STEPS, RG, C_PART), BF16),
            vmem((PLACES, 2, D_LAST, D), BF16),
            vmem((PLACES, 2, RG, C_PART), BF16),
            dma((*per_part, STEPS)),
            dma((*per_part, STEPS)),
            dma((PLACES, 2)),
            dma(per_part),
            dma((LAYERS, STEPS)),
            dma((LAYERS, PAIRS - D_PAIRS)),
            dma(two),
            dma((2,)),
            dma((2,)),
            dma((2, 5)),
            dma(two),
            dma(two),
            dma((3,)),
        ],
        compiler_params=pltpu.CompilerParams(
            collective_id=1, has_side_effects=True, vmem_limit_bytes=63 * 1024 * 1024
        ),
        name="backward_reduce",
    )(dy, x, h1, gathered_gu, gathered_d, p, q, actt, at)


def solution(mesh):
    def step(x, dy, wg, wu, wd):
        gu, d, p, q, actt, at, h1 = forward(x[0], wg, wu, wd)
        dx, dgu, dd, *_ = backward(dy[0], x[0], h1, gu, d, p, q, actt, at)
        return dx[None], dgu[0], dgu[1], dd

    both, rows = P(("rep", "dp"), None, None), P(None, "dp", None)
    own = P("rep", "dp", None)
    return jax.shard_map(
        step,
        mesh=mesh,
        in_specs=(both, both, rows, rows, rows),
        out_specs=(both, own, own, own),
        check_vma=False,
    )
```

time: 1660 us -> 537 us (0.32)
  waiting for transfers between devices: 1240 us -> 0 us
  Pallas kernels: 0 us -> 529 us
  matrix products: 283 us -> 0 us
  other arithmetic: 68.6 us -> 0 us
  local copies, waits for them, and re-layouts: 31.9 us -> 6.02 us
    unnamed x18 -> x0, waiting for transfers between devices: 901 us -> none
    pallas_call x0 -> x2, Pallas kernels: none -> 529 us  [the longest x1 326 us: backward(): pl.pallas_call(backward_kernel, out_shape=outs, in_specs=[any_] * 9, out_...]
    squeeze x6 -> x0, waiting for transfers between devices: 344 us -> none  [stack(): h = layer(h, {name: w[number] for name, w in weights.items()})]
    dot_general x17 -> x0, matrix products: 283 us -> none  [the longest x6 110 us: layer(): up = jnp.dot(a, w['w_up'], preferred_element_type=jnp.float32)]
    unnamed x5 -> x0, other arithmetic: 50 us -> none
    unnamed x43 -> x6, local copies, waits for them, and re-layouts: 25 us -> 2.87 us
  transfers between devices with their start and end apart: 12 -> 0, of which waited for: 12 -> 0; matrix products, arithmetic and copies ran while one was open for 17% -> 0% of each run, Pallas kernels for 0% -> 0%
where the time goes in v1:
time: 537 us; the launch traced here: 536 us
  Pallas kernels  529 us (99%)
  local copies, waits for them, and re-layouts  6.02 us (1%)
    pallas_call x1, Pallas kernels, backward(): pl.pallas_call(backward_kernel, out_shape=outs, in_specs=[any_] * 9, out_...  326 us
    pallas_call x1, Pallas kernels, forward(): pl.pallas_call(forward_kernel, out_shape=(jax.ShapeDtypeStruct((LAYERS, 2...  203 us

profile of v1, /device:TPU:0, one launch (start us, length us, event | category | flops | bytes accessed | tf_op | source)
XLA Modules:
  0.0 535.9 jit_solution(16161450640706683837)
XLA Ops:
  0.6 203.4 %forward_gather.1 = (bf16[2,2,896,4864]{3,2,1,0:T(8,128)(2,1)}, bf16[2,4864,896]{2,1,0:T(8,128)(2,1)}, f32[2,19,1024,256]{3,2,1,0:T(8,128)}, f32[2,19,1024,256]{...) custom-call(bf16[1024,896]{1,0:T(8,128)(2,1)} %bitcast.7, ...), custom_call_target="tpu_custom_call" | custom-call | tf_op jit(solution)/shard_map/forward_gather/pallas_call | solution.py:330
  204.0 325.8 %backward_reduce.1 = (bf16[1024,896]{1,0:T(8,128)(2,1)}, bf16[2,2,56,4736]{3,2,1,0:T(8,128)(2,1)}, bf16[2,296,896]{2,1,0:T(8,128)(2,1)}, bf16[2,2,8,56,4864]{4,3...) custom-call(bf16[1024,896]{1,0:T(8,128)(2,1)} %bitcast.9, ...), custom_call_target="tpu_custom_call" | custom-call | tf_op jit(solution)/shard_map/backward_reduce/pallas_call | solution.py:640
  529.8 0.0 copy-start
  529.8 3.1 slice_bitcast_fusion
  533.0 0.0 copy-done
  533.0 0.0 copy-start.1
  533.0 1.2 copy.11
  534.2 0.7 copy-done.1
  534.9 1.0 copy.12
Async XLA Ops:
  529.8 3.2 copy-start
  533.0 1.9 copy-start.1

commit v2 on v0

v2 whole, which is shorter than its diff:
```python
import functools

import jax
import jax.numpy as jnp
from jax import lax
from jax.experimental import pallas as pl
from jax.experimental.pallas import tpu as pltpu
from jax.sharding import PartitionSpec as P

MESH = pl.DeviceIdType.MESH
BF16, F32 = jnp.bfloat16, jnp.float32
LAYERS, T, D, FF = 2, 1024, 896, 4736
N = 16
TILE = 256
TILES = 19
FFP = TILE * TILES
RG, RD = D // N, FF // N
EPS = 1e-6
CH = 128
ROW_CHUNKS = 2
ROWS = T // ROW_CHUNKS

DOWN = 2
COLUMNS = {0: (0, 10), 1: (10, TILES)}
GU_A = {0: 7 * 128, 1: 5 * 128}
UNIT_KINDS = (0, 1, DOWN, 0, 1, DOWN)
UNITS, HOPS, ITEMS = len(UNIT_KINDS), 7, 2
LAYER_1 = 3
D_A = 96
D_B = RD - 2 * D_A
STAGGER = 4
PER_UNIT = STAGGER * 2 * ITEMS
READY = 2 * PER_UNIT + 1
N_PIECES = ((0, 512), (512, 384))


class Place:
    def __init__(self):
        self.rep = lax.axis_index("rep")
        me = lax.axis_index("dp")
        self.core = lax.rem(me, 2)
        self.chip = me // 2
        self.ring = jnp.where(self.chip < 4, self.chip, 11 - self.chip)
        self.way = 1 - 2 * self.core
        self.next = (self.rep, self.device(1))
        self.prev = (self.rep, self.device(-1))
        self.sibling = (self.rep, self.chip * 2 + 1 - self.core)
        self.other = (1 - self.rep, me)

    def chip_at(self, steps):
        r = lax.rem(self.ring + self.way * steps + 16, 8)
        return jnp.where(r < 4, r, 11 - r)

    def device(self, steps):
        return self.chip_at(steps) * 2 + self.core


def barrier(devices):
    sem = pltpu.get_barrier_semaphore()
    for device in devices:
        pl.semaphore_signal(sem, inc=1, device_id=device, device_id_type=MESH)
    pl.semaphore_wait(sem, len(devices))


def remote(src, dst, send, recv, device):
    return pltpu.make_async_remote_copy(
        src_ref=src, dst_ref=dst, send_sem=send, recv_sem=recv, device_id=device, device_id_type=MESH
    )


def loop(lo, hi, body):
    def run(i, carry):
        body(i)
        return carry

    lax.fori_loop(lo, hi, run, 0)


def start(copies):
    for copy in copies:
        copy.start()


def wait(copies):
    for copy in copies:
        copy.wait()


def mult(x, m):
    return pl.multiple_of(x, m)


def dot(a, b, dims=((1,), (0,))):
    return lax.dot_general(a, b, (dims, ((), ())), preferred_element_type=F32)


class Gather:
    def __init__(self, here, sources, g_out, d_out, sems):
        self.here, self.sources, self.g_out, self.d_out = here, sources, g_out, d_out
        self.ring_recv, self.x_recv, self.sib_recv, self.ring_send, self.x_send, self.sib_send = sems

    @staticmethod
    def columns(kind):
        first, end = COLUMNS[kind]
        return first * TILE, min(end * TILE, FF) - first * TILE

    def cut(self, kind, is_own, group):
        if kind == DOWN:
            return (pl.ds(mult(D_B + D_A * group, 8), D_A) if is_own else pl.ds(0, D_B)), pl.ds(0, D)
        first, size = self.columns(kind)
        common = size - 2 * GU_A[kind]
        if is_own:
            return pl.ds(0, RG), pl.ds(mult(first + common + GU_A[kind] * group, 128), GU_A[kind])
        return pl.ds(0, RG), pl.ds(first, common)

    def region(self, l, kind, dev, is_own, group):
        rows, cols = self.cut(kind, is_own, group)
        if kind == DOWN:
            return self.d_out.at[l, pl.ds(mult(dev * RD + rows.start, 8), rows.size), cols]
        return self.g_out.at[l, :, pl.ds(mult(dev * RG, 8), RG), cols]

    def send_ring(self, src, dst, u, t, item):
        return remote(src, dst, self.ring_send.at[u], self.ring_recv.at[u, t - 1, item], self.here.next)

    def send_x(self, reg, u, t):
        return remote(reg, reg, self.x_send.at[u], self.x_recv.at[u, t - 1], self.here.other)

    def send_sibling(self, src, dst, u):
        return remote(src, dst, self.sib_send.at[u], self.sib_recv.at[u], self.here.sibling)

    def start_own(self, u, l, kind):
        me = self.here.device(0)
        sources = [ref.at[l] for ref in (self.sources[2:] if kind == DOWN else self.sources[:2])]
        for item in range(ITEMS):
            rows, cols = self.cut(kind, item == 0, self.here.rep)
            to = self.region(l, kind, me, item == 0, self.here.rep)
            for m, src in enumerate(sources):
                self.send_ring(src.at[rows, cols], to if kind == DOWN else to.at[m], u, 1, item).start()
        for m, src in enumerate(sources):
            if kind == DOWN:
                self.send_sibling(src, self.d_out.at[l, pl.ds(mult(me * RD, 8), RD), :], u).start()
            else:
                cols = pl.ds(*self.columns(kind))
                to = self.g_out.at[l, m, pl.ds(mult(me * RG, 8), RG), cols]
                self.send_sibling(src.at[:, cols], to, u).start()

    def ring_event(self, u, l, kind, t, item):
        is_own = item == 0
        reg = self.region(l, kind, self.here.device(-t), is_own, self.here.rep)
        self.send_ring(reg, reg, u, t, item).wait_recv()
        pl.when(t < HOPS)(lambda: self.send_ring(reg, reg, u, t + 1, item).start())
        if is_own:
            self.send_x(reg, u, t).start()
        self.send_sibling(reg, reg, u).start()

    def x_event(self, u, l, kind, t):
        reg = self.region(l, kind, self.here.device(-t), True, 1 - self.here.rep)
        self.send_x(reg, u, t).wait_recv()
        self.send_sibling(reg, reg, u).start()

    def event(self, e):
        round_, place = e // (2 * ITEMS), lax.rem(e, 2 * ITEMS)
        newer, item = place // ITEMS, lax.rem(place, ITEMS)

        def at(round_):
            return (round_ + STAGGER) // STAGGER - 2 + newer, lax.rem(round_, STAGGER) + STAGGER * (1 - newer)

        def of_kind(u, kind):
            first, *others = [i for i in range(UNITS) if UNIT_KINDS[i] == kind]
            return functools.reduce(lambda so_far, i: so_far | (u == i), others, u == first)

        u, t = at(round_)
        l = jnp.where(u < LAYER_1, 0, 1)
        was, hop = at(round_ - 1)
        was_l = jnp.where(was < LAYER_1, 0, 1)
        crosses = (item == 0) & (hop > 0) & (round_ > 0)
        for kind in sorted(set(UNIT_KINDS)):

            @pl.when(of_kind(u, kind))
            def _(kind=kind):
                pl.when((t == 0) & (item == 0))(functools.partial(self.start_own, u, l, kind))
                for i in range(ITEMS):
                    pl.when((t > 0) & (item == i))(functools.partial(self.ring_event, u, l, kind, t, i))

            pl.when(crosses & of_kind(was, kind))(functools.partial(self.x_event, was, was_l, kind, hop))

    def events(self, lo, hi):
        loop(lo, hi, self.event)

    def whole(self, l, kind, of_gu, of_d):
        if kind == DOWN:
            return self.d_out.at[l, pl.ds(0, of_d), :]
        rows, width = of_gu
        return self.g_out.at[l, :, pl.ds(0, rows), pl.ds(0, width)]

    def wait_unit(self, u):
        kind, l = UNIT_KINDS[u], int(u >= LAYER_1)
        width = 0 if kind == DOWN else self.columns(kind)[1]
        half = self.whole(l, kind, (D // 2, width), FF // 2)
        self.send_sibling(half, half, u).wait_recv()

    def wait_sends(self, u):
        kind, l = UNIT_KINDS[u], int(u >= LAYER_1)
        width, own = (0, 0) if kind == DOWN else (self.columns(kind)[1], GU_A[kind])
        sent = (
            self.whole(l, kind, (HOPS * RG, width - own), HOPS * (D_A + D_B)),
            self.whole(l, kind, (HOPS * RG, own), HOPS * D_A),
            self.whole(l, kind, (D // 2, width), FF // 2),
        )
        for ref, sem in zip(sent, (self.ring_send, self.x_send, self.sib_send)):
            remote(ref, ref, sem.at[u], sem.at[u], self.here.next).wait_send()


def along(k, points):
    out = points[-1][1]
    for (k0, e0), (k1, e1) in reversed(list(zip(points, points[1:]))):
        out = jnp.where(k < k1, e0 + (k - k0) * (e1 - e0) // (k1 - k0), out)
    return out


TILE_POINTS = (
    ((0, 0), (20, PER_UNIT), (2 * TILES, 2 * PER_UNIT)),
    ((0, 3 * PER_UNIT), (20, 4 * PER_UNIT), (2 * TILES, 4 * PER_UNIT + 12)),
)
FORWARD_END = READY + TILE_POINTS[1][-1][1]
GATHER_END = READY + (UNITS - 1) * PER_UNIT


def forward_pass(
    here, gather, x_ref, g_out, d_out, p_out, q_out, actt_out, at_out, h1_out, local_sem, w_sem, o_sem, wd_sem, at_sem,
    a_s, h_s, at_s, prod_s, wd_s, wgu_t, p_s, q_s, pt_s, zc, zr,
):
    load_x = pltpu.make_async_copy(x_ref, h_s, at_sem.at[0])
    load_x.start()
    gather.events(ITEMS, 2 * ITEMS)
    zc[...] = jnp.zeros_like(zc)
    zr[...] = jnp.zeros_like(zr)
    me = here.device(0)
    wg_ref, wu_ref, wd_ref = gather.sources
    locals_ = []
    for l in range(LAYERS):
        for m in range(2):
            locals_.append((zc, g_out.at[l, m, :, pl.ds(FF, FFP - FF)]))
            locals_.append(((wg_ref, wu_ref)[m].at[l], g_out.at[l, m, pl.ds(mult(me * RG, 8), RG), pl.ds(0, FF)]))
        locals_.append((zr, d_out.at[l, pl.ds(FF, FFP - FF), :]))
        locals_.append((wd_ref.at[l], d_out.at[l, pl.ds(mult(me * RD, 8), RD), :]))
    locals_ = [pltpu.make_async_copy(src, dst, local_sem.at[i]) for i, (src, dst) in enumerate(locals_)]
    start(locals_)
    load_x.wait()

    def put_at(l):
        return pltpu.make_async_copy(at_s, at_out.at[l], at_sem.at[0])

    put_h = pltpu.make_async_copy(h_s, h1_out, at_sem.at[1])

    def norm(l, first_event, count):
        def chunk(i):
            rows = pl.ds(mult(i * CH, CH), CH)
            wide = h_s[rows, :].astype(F32)
            a = (wide * lax.rsqrt(jnp.mean(wide * wide, -1, keepdims=True) + EPS)).astype(BF16)
            a_s[rows, :] = a
            at_s[:, rows] = a.T
            gather.events(first_event + i * count, first_event + (i + 1) * count)

        loop(0, T // CH, chunk)
        put_at(l).start()

    def add_mlp(first_event):
        parts = [
            pltpu.make_async_copy(d_out.at[0, :, pl.ds(*piece)], wd_s.at[:, pl.ds(*piece)], wd_sem.at[i])
            for i, piece in enumerate(N_PIECES)
        ]
        start(parts)
        for i, piece in enumerate(N_PIECES):
            parts[i].wait()
            cols = pl.ds(*piece)

            def rows_part(r):
                rows = pl.ds(mult(r * ROWS, ROWS), ROWS)
                y = dot(prod_s[rows, :], wd_s[:, cols]).astype(BF16).astype(F32)
                h_s[rows, cols] = (h_s[rows, cols].astype(F32) + y).astype(BF16)
                now = first_event + (i * ROW_CHUNKS + r) * ITEMS
                gather.events(now, now + ITEMS)

            loop(0, ROW_CHUNKS, rows_part)

    def layer(l):
        def loads(j, slot):
            cols = pl.ds(mult(j * TILE, TILE), TILE)
            return [
                pltpu.make_async_copy(
                    g_out.at[l, m, :, cols], wgu_t.at[slot, :, pl.ds(m * TILE, TILE)], w_sem.at[slot, m]
                )
                for m in range(2)
            ]

        def stores(j, slot):
            rows = pl.ds(mult(j * TILE, TILE), TILE)
            pairs = ((p_s, p_out.at[l, j]), (q_s, q_out.at[l, j]), (pt_s, actt_out.at[l, rows, :]))
            return [pltpu.make_async_copy(src.at[slot], dst, o_sem.at[slot, i]) for i, (src, dst) in enumerate(pairs)]

        def done_by(k):
            return READY + jnp.where(l == 0, along(k, TILE_POINTS[0]), along(k, TILE_POINTS[1]))

        firsts = {u: COLUMNS[kind][0] for u, kind in enumerate(UNIT_KINDS) if kind != DOWN}

        def tick(j):
            slot = lax.rem(j, 2)
            for u, first in firsts.items():

                @pl.when((j == first) & ((l == 0) == (u < LAYER_1)))
                def _(u=u):
                    gather.wait_unit(u)

            is_first, next_is_first = ((k == 0) | (k == COLUMNS[1][0]) for k in (j, j + 1))
            pl.when(is_first)(lambda: start(loads(j, slot)))
            pl.when((j + 1 < TILES) & ~next_is_first)(lambda: start(loads(j + 1, 1 - slot)))
            wait(loads(j, slot))
            pl.when(j >= 2)(lambda: wait(stores(j - 2, slot)))

            def row_chunk(r):
                rows = pl.ds(mult(r * ROWS, ROWS), ROWS)
                both = dot(a_s[rows, :], wgu_t[slot])
                gate, up = both[:, :TILE], both[:, TILE:]
                s = 0.5 * jnp.tanh(0.5 * gate) + 0.5
                q = gate * s
                q_s[slot, rows, :] = q
                p_s[slot, rows, :] = up * (s + q * (1 - s))
                prod = (q * up).astype(BF16)
                pt_s[slot, :, rows] = prod.T
                prod_s[rows, pl.ds(mult(j * TILE, TILE), TILE)] = prod
                gather.events(done_by(2 * j + r), done_by(2 * j + r + 1))

            loop(0, ROW_CHUNKS, row_chunk)
            start(stores(j, slot))

        loop(0, TILES, tick)
        for j in (TILES - 2, TILES - 1):
            wait(stores(j, j % 2))

        @pl.when(l == 0)
        def _():
            gather.wait_unit(UNIT_KINDS.index(DOWN))
            now = READY + 2 * PER_UNIT
            put_at(0).wait()
            add_mlp(now)
            now += ITEMS * ROW_CHUNKS * len(N_PIECES)
            norm(1, now, 1)
            put_h.start()

    norm(0, 2 * ITEMS, 1)
    gather.events(2 * ITEMS + T // CH, READY)
    wait(locals_)
    loop(0, LAYERS, layer)
    put_h.wait()
    put_at(1).wait()


PAIRS, STEPS, PLACES = 4, 8, 4
PER_PAIR = STEPS // 2 * PLACES
QUEUE = LAYERS * PAIRS + 1
SECOND = PAIRS + 1
D_PARTS = ((0, 152), (152, 144))
BIG = 2 * TILE
BIGS = (TILES + 1) // 2
PART_BIGS = 3
C_PART = PART_BIGS * BIG
C_LAST = FF - 2 * C_PART
LAST_EVENT = (QUEUE + 1) * PER_PAIR
AHEAD = PLACES - 1
LAG = 2 * PLACES
BEFORE, BETWEEN, AFTER = (2, 63), (12, 74), (63, 120)


def backward_pass(
    here, gather, dy_ref, x_ref, h1_ref, g_ref, d_ref, p_ref, q_ref, actt_ref, at_ref,
    dx_out, dg_out, du_out, dd_out, own_gu, sib_gu, own_d, sib_d, slot_d, slot_c,
    red_recv, red_send, st_sem, fin_sem, sd_recv, sgu_recv, lhs_sem, blk_sem, blk_send, w_sem, term_sem, term_send, misc_sem,
    dh_s, at_s, h_s, dacc, lhs_t, blk_s, wgu_t, wd_t, p_t, q_t, dz_s, term_s, st_d, st_c,
):
    def chips(s):
        return here.chip_at(-1 - s), here.chip_at(1 + s)

    class Lane:
        def __init__(self, l, pair, lane, s, place, down, last):
            chip, _ = chips(s)
            self.s, self.place, self.lane = s, place, lane
            self.sems = [sem.at[l, pair, lane] for sem in (red_recv, red_send)]
            self.fin = fin_sem.at[l, pair, lane]
            if down:
                first, size = D_PARTS[last]
                rows, cut = pl.ds(first, size), pl.ds(0, size)
                self.slots = [slot_d.at[lane, to, cut, :] for to in (s, s + 1)]
                self.st = [st_d.at[place, i, cut, :] for i in range(2)]
                self.terms = [ref.at[l, chip, rows, :] for ref in (own_d, sib_d)]
                self.result = dd_out.at[l, rows, :]
            else:
                part = pair - 1
                cols, cut = (pl.ds(first, C_LAST if last else C_PART) for first in (mult(part * C_PART, 128), 0))
                self.slots = [slot_c.at[part, lane, to, :, cut] for to in (s, s + 1)]
                self.st = [st_c.at[place, i, :, cut] for i in range(2)]
                self.terms = [ref.at[l, lane, chip, :, cols] for ref in (own_gu, sib_gu)]
                self.result = [out.at[l, :, cols] for out in (dg_out, du_out)]

        def stage(self):
            pairs = zip(self.terms, self.st)
            return [pltpu.make_async_copy(a, b, st_sem.at[self.place, i]) for i, (a, b) in enumerate(pairs)]

        def send(self, to):
            recv, sent = self.sems
            return remote(self.slots[0], self.slots[to], sent.at[self.s], recv.at[self.s + to], here.next)

        def finish(self, action):
            if not isinstance(self.result, list):
                action(pltpu.make_async_copy(self.slots[0], self.result, self.fin))
                return
            for lane, result in enumerate(self.result):
                copy = pltpu.make_async_copy(self.slots[0], result, self.fin)
                pl.when(self.lane == lane)(functools.partial(action, copy))

        def step(self):
            wait(self.stage())
            slot = self.slots[0]
            ends = [st[...].astype(F32) for st in self.st]

            @pl.when(self.s > 0)
            def _():
                self.send(0).wait_recv()
                slot[...] = (slot[...].astype(F32) + (ends[0] + ends[1])).astype(BF16)

            @pl.when(self.s == 0)
            def _():
                slot[...] = (ends[0] + ends[1]).astype(BF16)

            pl.when(self.s < STEPS - 1)(lambda: self.send(1).start())
            pl.when(self.s == STEPS - 1)(lambda: self.finish(lambda copy: copy.start()))

        def wait_out(self):
            pl.when(self.s < STEPS - 1)(lambda: self.send(1).wait_send())
            pl.when(self.s == STEPS - 1)(lambda: self.finish(lambda copy: copy.wait()))

        def prefetch(self):
            start(self.stage())

    def with_lane(e, action, ahead_of=lambda l, pair, lane, s: None):
        round_, place = e // PLACES, lax.rem(e, PLACES)
        new = place // 2
        index = round_ // PLACES + new - 1
        s = lax.rem(round_, PLACES) + PLACES * (1 - new)
        lane = lax.rem(place, 2)

        @pl.when((index >= 0) & (index < QUEUE) & (index != 1))
        def _():
            second = jnp.where(index < SECOND, 0, 1)
            free = jnp.where((index > 1) & (index < SECOND), 1, 0)
            l, pair = 1 - second, index - SECOND * second - free
            ahead_of(l, pair, lane, s)
            for is_down, is_last, chosen in (
                (True, False, (pair == 0) & (lane == 0)), (True, True, (pair == 0) & (lane == 1)),
                (False, False, (pair > 0) & (pair < PAIRS - 1)), (False, True, pair == PAIRS - 1),
            ):
                pl.when(chosen)(lambda: action(Lane(l, pair, lane, s, place, is_down, is_last)))

    def terms_ready(l, pair, lane, s):
        @pl.when((pair == 0) & (lane == 0))
        def _():
            whole = sib_d.at[l, 0]
            remote(whole, whole, blk_send.at[0], sd_recv.at[l, s], here.sibling).wait_recv()

        @pl.when((pair > 0) & (lane == 0) & (s == 0))
        def _():
            for is_last in (False, True):
                width = FFP - 2 * C_PART if is_last else C_PART

                @pl.when((pair == PAIRS - 1) == is_last)
                def _(width=width):
                    part = sib_gu.at[l, :, :, :, pl.ds(0, width)]
                    sem = sgu_recv.at[l, pair - 1]
                    remote(part, part, term_send.at[0, 0], sem, here.sibling).wait_recv()

    def events(lo, hi):
        loop(lo, hi, event)

    def fetch(e):
        with_lane(e, Lane.prefetch, terms_ready)

    def event(e):
        pl.when(e >= LAG)(lambda: with_lane(e - LAG, Lane.wait_out))
        fetch(e + AHEAD)
        with_lane(e, Lane.step)

    def lhs_loads(l, s, slot):
        mine, other = chips(s)
        rows = ((mine * 2 + here.core) * RD, (other * 2 + 1 - here.core) * RD)
        return [
            pltpu.make_async_copy(actt_ref.at[l, pl.ds(mult(row, 8), RD), :], lhs_t.at[slot, i], lhs_sem.at[slot, i])
            for i, row in enumerate(rows)
        ]

    def block_copies(l, s, slot):
        mine, other = chips(s)
        return (
            pltpu.make_async_copy(blk_s.at[slot, 0], own_d.at[l, mine], blk_sem.at[slot]),
            remote(blk_s.at[slot, 1], sib_d.at[l, other], blk_send.at[slot], sd_recv.at[l, s], here.sibling),
        )

    def both_halves(j, action):
        action(0)
        pl.when(j < BIGS - 1)(lambda: action(1))

    def tile_loads(l, j, slot, half):
        tile = 2 * j + half
        src = pl.ds(mult(tile * TILE, TILE), TILE)
        dst = pl.ds(half * TILE, TILE)
        pairs = [
            (d_ref.at[l, src, :], wd_t.at[slot, dst, :]),
            (p_ref.at[l, tile], p_t.at[slot, :, dst]),
            (q_ref.at[l, tile], q_t.at[slot, :, dst]),
        ]
        pairs += [(g_ref.at[l, m, :, src], wgu_t.at[slot, :, pl.ds((2 * half + m) * TILE, TILE)]) for m in range(2)]
        return [pltpu.make_async_copy(src, dst, w_sem.at[slot, half, i]) for i, (src, dst) in enumerate(pairs)]

    def term_copies(l, j, half):
        cols = pl.ds(mult((2 * j + half) * TILE, TILE), TILE)
        part = jnp.minimum(j // PART_BIGS, PAIRS - 2)
        own, sib = [], []
        for m in range(2):
            mine, other = term_s.at[half, m, :, here.core], term_s.at[half, m, :, 1 - here.core]
            own.append(pltpu.make_async_copy(mine, own_gu.at[l, m, :, :, cols], term_sem.at[half, m]))
            to = sib_gu.at[l, m, :, :, cols]
            sib.append(remote(other, to, term_send.at[half, m], sgu_recv.at[l, part], here.sibling))
        return own, sib

    def start_terms(l, j, half):
        own, sib = term_copies(l, j, half)
        start(own + sib)

    def wait_terms(l, j, half):
        own, sib = term_copies(l, j, half)
        wait(own)
        for copy in sib:
            copy.wait_send()

    def wait_block(l, s, slot):
        own, sib = block_copies(l, s, slot)
        own.wait()
        sib.wait_send()

    def layer(i):
        l = 1 - i
        before, between, after = (jnp.where(i == 0, *counts) for counts in (BEFORE, BETWEEN, AFTER))
        load_at = pltpu.make_async_copy(at_ref.at[l], at_s, misc_sem.at[0])
        load_at.start()
        pl.when(i == 0)(pltpu.make_async_copy(h1_ref, h_s, misc_sem.at[1]).start)
        pl.when(i == 1)(pltpu.make_async_copy(x_ref, h_s, misc_sem.at[1]).start)
        start(lhs_loads(l, 0, 0))
        first_loads = lambda: both_halves(0, lambda half: start(tile_loads(l, 0, 0, half)))
        pl.when(i == 1)(first_loads)

        def pair(s):
            slot = lax.rem(s, 2)
            pl.when(s < STEPS - 1)(lambda: start(lhs_loads(l, s + 1, 1 - slot)))
            wait(lhs_loads(l, s, slot))
            for b in range(2):
                blk_s[slot, b] = dot(lhs_t[slot, b], dh_s[...]).astype(BF16)
            start(block_copies(l, s, slot))

            @pl.when(i == 0)
            def _():
                lo, hi = (FORWARD_END + (GATHER_END - FORWARD_END) * to // STEPS for to in (s, s + 1))
                gather.events(lo, hi)

            pl.when(s >= 1)(lambda: wait_block(l, s - 1, 1 - slot))
            pl.when((i == 0) & (s == 1))(lambda: loop(BEFORE[0], BEFORE[0] + AHEAD, fetch))

            def done_by(s):
                cap = jnp.where(i == 0, jnp.maximum(PLACES * s - 1, before), LAST_EVENT)
                return jnp.minimum(before + ((between - before) * (s + 1)) // STEPS, cap)

            loop(jnp.where(s == 0, before, done_by(s - 1)), done_by(s), event)

        loop(0, STEPS, pair)
        wait_block(l, STEPS - 1, (STEPS - 1) % 2)

        @pl.when(i == 0)
        def _():
            gather.wait_unit(UNITS - 1)
            first_loads()

        load_at.wait()
        dacc[...] = jnp.zeros_like(dacc)

        def tick(j):
            slot = lax.rem(j, 2)
            pl.when(j + 1 < BIGS)(lambda: both_halves(j + 1, lambda half: start(tile_loads(l, j + 1, 1 - slot, half))))
            both_halves(j, lambda half: wait(tile_loads(l, j, slot, half)))

            @pl.when(j == BIGS - 1)
            def _():
                for ref in (p_t, q_t):
                    ref[slot, :, pl.ds(TILE, TILE)] = jnp.zeros((T, TILE), F32)

            def done_by(k):
                ready = jnp.maximum(k - 2, 0) // (PART_BIGS * 4)
                cap = jnp.where(i == 0, PER_PAIR * (2 + jnp.minimum(ready, PAIRS - 2)) - 1, LAST_EVENT)
                return jnp.minimum(between + (k * (after - between)) // (4 * BIGS), cap)

            def quarter(k):
                events(done_by(4 * j + k), done_by(4 * j + k + 1))

            for r in range(2):
                rows = pl.ds(r * ROWS, ROWS)
                dprod = dot(dh_s[rows, :], wd_t[slot], ((1,), (1,))).astype(BF16).astype(F32)
                by_gate = (dprod * p_t[slot, rows, :]).astype(BF16)
                by_up = (dprod * q_t[slot, rows, :]).astype(BF16)
                for half in range(2):
                    for m, by in enumerate((by_gate, by_up)):
                        part = by[:, half * TILE : (half + 1) * TILE]
                        dz_s[rows, pl.ds((2 * half + m) * TILE, TILE)] = part
                dacc[rows, :] += dot(dz_s[rows, :], wgu_t[slot], ((1,), (1,)))
                if r == 1:
                    pl.when(j > 0)(lambda: [wait_terms(l, j - 1, half) for half in range(2)] and None)
                quarter(r)
            for r in range(2):
                term = dot(at_s[pl.ds(r * D // 2, D // 2), :], dz_s[...])
                for b in range(8):
                    for half in range(2):
                        for m in range(2):
                            col = (2 * half + m) * TILE
                            block = term[b * RG : (b + 1) * RG, col : col + TILE]
                            term_s[half, m, r * 4 + b // 2, b % 2] = block.astype(BF16)
                if r == 1:
                    both_halves(j, lambda half: start_terms(l, j, half))
                quarter(2 + r)

        loop(0, BIGS, tick)
        wait_terms(l, BIGS - 1, 0)
        pltpu.make_async_copy(h1_ref, h_s, misc_sem.at[1]).wait()

        def new_dh(r):
            rows = pl.ds(mult(r * CH, CH), CH)
            da = dacc[rows, :].astype(BF16).astype(F32)
            wide = h_s[rows, :].astype(F32)
            scale = lax.rsqrt(jnp.mean(wide * wide, -1, keepdims=True) + EPS)
            along = jnp.mean(da * wide, -1, keepdims=True) * scale * scale
            by_h = (scale * (da - wide * along)).astype(BF16).astype(F32)
            dh_s[rows, :] = (dh_s[rows, :].astype(F32) + by_h).astype(BF16)

        loop(0, T // CH, new_dh)

    load_dy = pltpu.make_async_copy(dy_ref, dh_s, misc_sem.at[2])
    load_dy.start()
    load_dy.wait()
    loop(0, LAYERS, layer)
    put_dx = pltpu.make_async_copy(dh_s, dx_out, misc_sem.at[2])
    put_dx.start()
    loop(AFTER[1], LAST_EVENT, event)
    loop(LAST_EVENT - LAG, LAST_EVENT, lambda e: with_lane(e, Lane.wait_out))
    put_dx.wait()


def kernel(
    dy_ref, x_ref, wg_ref, wu_ref, wd_ref,
    dx_out, dg_out, du_out, dd_out, own_gu, sib_gu, own_d, sib_d, g_out, d_out, p_out, q_out, actt_out, at_out, h1_out,
    slot_d, slot_c, *sems,
):
    gather_sems, forward_sems, backward_sems = sems[:6], sems[6:11], sems[11:]
    here = Place()
    barrier((here.next, here.prev, here.sibling, here.other))
    gather = Gather(here, (wg_ref, wu_ref, wd_ref), g_out, d_out, gather_sems)
    vmem = pltpu.VMEM
    two = (2, 2)
    pl.run_scoped(
        functools.partial(
            forward_pass, here, gather, x_ref, g_out, d_out, p_out, q_out, actt_out, at_out, h1_out, *forward_sems
        ),
        vmem((T, D), BF16),
        vmem((T, D), BF16),
        vmem((D, T), BF16),
        vmem((T, FFP), BF16),
        vmem((FFP, D), BF16),
        vmem((2, D, 2 * TILE), BF16),
        vmem((2, T, TILE), F32),
        vmem((2, T, TILE), F32),
        vmem((2, TILE, T), BF16),
        vmem((D, FFP - FF), BF16),
        vmem((FFP - FF, D), BF16),
    )
    pl.run_scoped(
        functools.partial(
            backward_pass, here, gather, dy_ref, x_ref, h1_out, g_out, d_out, p_out, q_out, actt_out, at_out,
            dx_out, dg_out, du_out, dd_out, own_gu, sib_gu, own_d, sib_d, slot_d, slot_c, *backward_sems,
        ),
        vmem((T, D), BF16),
        vmem((D, T), BF16),
        vmem((T, D), BF16),
        vmem((T, D), F32),
        vmem((*two, RD, T), BF16),
        vmem((*two, RD, D), BF16),
        vmem((2, D, 2 * BIG), BF16),
        vmem((2, BIG, D), BF16),
        vmem((2, T, BIG), F32),
        vmem((2, T, BIG), F32),
        vmem((T, 2 * BIG), BF16),
        vmem((*two, 8, 2, RG, TILE), BF16),
        vmem((PLACES, 2, D_PARTS[0][1], D), BF16),
        vmem((PLACES, 2, RG, C_LAST), BF16),
    )
    for u in range(UNITS):
        gather.wait_sends(u)


def both_passes(dy, x, wg, wu, wd):
    any_, vmem = pl.BlockSpec(memory_space=pl.ANY), pl.BlockSpec(memory_space=pltpu.VMEM)
    dma = pltpu.SemaphoreType.DMA
    shape = jax.ShapeDtypeStruct
    two = (2, 2)
    per_part = (LAYERS, PAIRS, 2)
    outs = (
        shape((T, D), BF16),
        *[shape((LAYERS, RG, FF), BF16)] * 2,
        shape((LAYERS, RD, D), BF16),
        *[shape((LAYERS, 2, 8, RG, FFP), BF16)] * 2,
        *[shape((LAYERS, 8, RD, D), BF16)] * 2,
        shape((LAYERS, 2, D, FFP), BF16),
        shape((LAYERS, FFP, D), BF16),
        *[shape((LAYERS, TILES, T, TILE), F32)] * 2,
        shape((LAYERS, FFP, T), BF16),
        shape((LAYERS, D, T), BF16),
        shape((T, D), BF16),
    )
    gather_sems = [dma((UNITS, HOPS, ITEMS)), dma((UNITS, HOPS)), *[dma((UNITS,))] * 4]
    forward_sems = [dma((LAYERS * 6,)), dma(two), dma((2, 3)), dma((2,)), dma((2,))]
    backward_sems = [
        dma((*per_part, STEPS)),
        dma((*per_part, STEPS)),
        dma((PLACES, 2)),
        dma(per_part),
        dma((LAYERS, STEPS)),
        dma((LAYERS, PAIRS - 1)),
        dma(two),
        dma((2,)),
        dma((2,)),
        dma((*two, 5)),
        dma(two),
        dma(two),
        dma((3,)),
    ]
    return pl.pallas_call(
        kernel,
        out_shape=outs,
        in_specs=[any_] * 2 + [vmem] * 3,
        out_specs=(any_,) * len(outs),
        scratch_shapes=[
            pltpu.VMEM((2, STEPS, D_PARTS[0][1], D), BF16),
            pltpu.VMEM((PAIRS - 1, 2, STEPS, RG, C_LAST), BF16),
            *gather_sems,
            *forward_sems,
            *backward_sems,
        ],
        compiler_params=pltpu.CompilerParams(
            collective_id=0, has_side_effects=True, vmem_limit_bytes=63 * 1024 * 1024
        ),
        name="both_passes",
    )(dy, x, wg, wu, wd)


def solution(mesh):
    def step(x, dy, wg, wu, wd):
        dx, dg, du, dd, *_ = both_passes(dy[0], x[0], wg, wu, wd)
        return dx[None], dg, du, dd

    both, rows = P(("rep", "dp"), None, None), P(None, "dp", None)
    own = P("rep", "dp", None)
    return jax.shard_map(
        step,
        mesh=mesh,
        in_specs=(both, both, rows, rows, rows),
        out_specs=(both, own, own, own),
        check_vma=False,
    )
```

time: 1660 us -> 497 us (0.30)
  waiting for transfers between devices: 1240 us -> 0 us
  Pallas kernels: 0 us -> 489 us
  matrix products: 283 us -> 0 us
  other arithmetic: 68.6 us -> 0 us
  local copies, waits for them, and re-layouts: 31.9 us -> 6.53 us
    unnamed x18 -> x0, waiting for transfers between devices: 901 us -> none
    pallas_call x0 -> x1, Pallas kernels: none -> 489 us  [both_passes(): pl.pallas_call(kernel, out_shape=outs, in_specs=[any_] * 2 + [vmem] * 3,...]
    squeeze x6 -> x0, waiting for transfers between devices: 344 us -> none  [stack(): h = layer(h, {name: w[number] for name, w in weights.items()})]
    dot_general x17 -> x0, matrix products: 283 us -> none  [the longest x6 110 us: layer(): up = jnp.dot(a, w['w_up'], preferred_element_type=jnp.float32)]
    unnamed x5 -> x0, other arithmetic: 50 us -> none
    unnamed x43 -> x10, local copies, waits for them, and re-layouts: 25 us -> 6.53 us
  transfers between devices with their start and end apart: 12 -> 0, of which waited for: 12 -> 0; matrix products, arithmetic and copies ran while one was open for 17% -> 0% of each run, Pallas kernels for 0% -> 0%
where the time goes in v2:
time: 497 us; the launch traced here: 496 us
  Pallas kernels  489 us (98%)
  local copies, waits for them, and re-layouts  6.53 us (1%)
    pallas_call x1, Pallas kernels, both_passes(): pl.pallas_call(kernel, out_shape=outs, in_specs=[any_] * 2 + [vmem] * 3,...  489 us

profile of v2, /device:TPU:0, one launch (start us, length us, event | category | flops | bytes accessed | tf_op | source)
XLA Modules:
  0.0 495.8 jit_solution(9160786379460528494)
XLA Ops:
  0.6 488.6 %both_passes.1 = (bf16[1024,896]{1,0:T(8,128)(2,1)}, bf16[2,56,4736]{2,1,0:T(8,128)(2,1)}, bf16[2,56,4736]{2,1,0:T(8,128)(2,1)}, bf16[2,296,896]{2,1,0:T(8,128)(...) custom-call(bf16[1024,896]{1,0:T(8,128)(2,1)} %bitcast.4, ...), custom_call_target="tpu_custom_call" | custom-call | tf_op jit(solution)/shard_map/both_passes/pallas_call | solution.py:749
  489.3 0.0 copy-start.2
  489.3 3.0 copy.13
  492.3 0.0 copy-done.2
  492.3 0.0 copy-start.1
  492.3 0.0 copy-start
  492.3 1.0 copy.14
  493.2 0.6 copy-done.1
  493.9 1.0 copy.15
  494.8 0.0 copy-done
  494.8 1.0 copy.16
Async XLA Ops:
  489.3 3.0 copy-start.2
  492.3 1.6 copy-start.1
  492.3 2.6 copy-start

commit v3 on v2

--- a/solution.py
+++ b/solution.py
@@ -21,8 +21,8 @@
 ROWS = T // ROW_CHUNKS
 
 DOWN = 2
-COLUMNS = {0: (0, 10), 1: (10, TILES)}
-GU_A = {0: 7 * 128, 1: 5 * 128}
+COLUMNS = {0: (0, 12), 1: (12, TILES)}
+GU_A = {0: 8 * 128, 1: 4 * 128}
 UNIT_KINDS = (0, 1, DOWN, 0, 1, DOWN)
 UNITS, HOPS, ITEMS = len(UNIT_KINDS), 7, 2
 LAYER_1 = 3
@@ -219,8 +219,8 @@
 
 
 TILE_POINTS = (
-    ((0, 0), (20, PER_UNIT), (2 * TILES, 2 * PER_UNIT)),
-    ((0, 3 * PER_UNIT), (20, 4 * PER_UNIT), (2 * TILES, 4 * PER_UNIT + 12)),
+    ((0, 0), (24, PER_UNIT), (2 * TILES, 2 * PER_UNIT)),
+    ((0, 3 * PER_UNIT), (24, 4 * PER_UNIT), (2 * TILES, 4 * PER_UNIT + 10)),
 )
 FORWARD_END = READY + TILE_POINTS[1][-1][1]
 GATHER_END = READY + (UNITS - 1) * PER_UNIT
@@ -228,13 +228,14 @@
 
 def forward_pass(
     here, gather, x_ref, g_out, d_out, p_out, q_out, actt_out, at_out, h1_out, local_sem, w_sem, o_sem, wd_sem, at_sem,
-    a_s, h_s, at_s, prod_s, wd_s, wgu_t, p_s, q_s, pt_s, zc, zr,
+    a_s, h_s, at_s, prod_s, wd_s, wgu_t, both_s, p_s, q_s, pt_s, zc, zr,
 ):
     load_x = pltpu.make_async_copy(x_ref, h_s, at_sem.at[0])
     load_x.start()
     gather.events(ITEMS, 2 * ITEMS)
     zc[...] = jnp.zeros_like(zc)
     zr[...] = jnp.zeros_like(zr)
+    both_s[...] = jnp.zeros_like(both_s)
     me = here.device(0)
     wg_ref, wu_ref, wd_ref = gather.sources
     locals_ = []
@@ -316,26 +317,31 @@
             pl.when(is_first)(lambda: start(loads(j, slot)))
             pl.when((j + 1 < TILES) & ~next_is_first)(lambda: start(loads(j + 1, 1 - slot)))
             wait(loads(j, slot))
-            pl.when(j >= 2)(lambda: wait(stores(j - 2, slot)))
-
-            def row_chunk(r):
-                rows = pl.ds(mult(r * ROWS, ROWS), ROWS)
-                both = dot(a_s[rows, :], wgu_t[slot])
-                gate, up = both[:, :TILE], both[:, TILE:]
-                s = 0.5 * jnp.tanh(0.5 * gate) + 0.5
-                q = gate * s
-                q_s[slot, rows, :] = q
-                p_s[slot, rows, :] = up * (s + q * (1 - s))
-                prod = (q * up).astype(BF16)
-                pt_s[slot, :, rows] = prod.T
-                prod_s[rows, pl.ds(mult(j * TILE, TILE), TILE)] = prod
+            before = jnp.maximum(j - 1, 0)
+            for r in range(ROW_CHUNKS):
+                hidden(1 - r, j if r else before, slot if r else 1 - slot)
+                both_s[r] = dot(a_s[pl.ds(r * ROWS, ROWS), :], wgu_t[slot])
+                if r == 0:
+                    pl.when(j >= 1)(lambda: start(stores(j - 1, 1 - slot)))
+                    pl.when(j >= 2)(lambda: wait(stores(j - 2, slot)))
                 gather.events(done_by(2 * j + r), done_by(2 * j + r + 1))
 
-            loop(0, ROW_CHUNKS, row_chunk)
-            start(stores(j, slot))
+        def hidden(r, j, slot):
+            rows = pl.ds(r * ROWS, ROWS)
+            gate, up = both_s[r, :, pl.ds(0, TILE)], both_s[r, :, pl.ds(TILE, TILE)]
+            s = 0.5 * jnp.tanh(0.5 * gate) + 0.5
+            q = gate * s
+            q_s[slot, rows, :] = q
+            p_s[slot, rows, :] = up * (s + q * (1 - s))
+            prod = (q * up).astype(BF16)
+            pt_s[slot, :, rows] = prod.T
+            prod_s[rows, pl.ds(mult(j * TILE, TILE), TILE)] = prod
 
         loop(0, TILES, tick)
-        for j in (TILES - 2, TILES - 1):
+        last = TILES - 1
+        hidden(1, last, last % 2)
+        start(stores(last, last % 2))
+        for j in (last - 1, last):
             wait(stores(j, j % 2))
 
         @pl.when(l == 0)
@@ -366,6 +372,7 @@
 PART_BIGS = 3
 C_PART = PART_BIGS * BIG
 C_LAST = FF - 2 * C_PART
+D_PIECE, C_PIECE = 72, 6 * 128
 LAST_EVENT = (QUEUE + 1) * PER_PAIR
 AHEAD = PLACES - 1
 LAG = 2 * PLACES
@@ -390,14 +397,21 @@
             if down:
                 first, size = D_PARTS[last]
                 rows, cut = pl.ds(first, size), pl.ds(0, size)
-                self.slots = [slot_d.at[lane, to, cut, :] for to in (s, s + 1)]
+                pieces = [pl.ds(0, D_PIECE), pl.ds(D_PIECE, size - D_PIECE)]
+                self.slot = slot_d.at[lane, s, cut, :]
+                self.slots = [[slot_d.at[lane, to, piece, :] for to in (s, s + 1)] for piece in pieces]
+                self.ends = [[st_d.at[place, i, piece, :] for i in range(2)] for piece in pieces]
                 self.st = [st_d.at[place, i, cut, :] for i in range(2)]
                 self.terms = [ref.at[l, chip, rows, :] for ref in (own_d, sib_d)]
                 self.result = dd_out.at[l, rows, :]
             else:
                 part = pair - 1
-                cols, cut = (pl.ds(first, C_LAST if last else C_PART) for first in (mult(part * C_PART, 128), 0))
-                self.slots = [slot_c.at[part, lane, to, :, cut] for to in (s, s + 1)]
+                size = C_LAST if last else C_PART
+                cols, cut = (pl.ds(first, size) for first in (mult(part * C_PART, 128), 0))
+                pieces = [pl.ds(0, C_PIECE), pl.ds(C_PIECE, size - C_PIECE)]
+                self.slot = slot_c.at[part, lane, s, :, cut]
+                self.slots = [[slot_c.at[part, lane, to, :, piece] for to in (s, s + 1)] for piece in pieces]
+                self.ends = [[st_c.at[place, i, :, piece] for i in range(2)] for piece in pieces]
                 self.st = [st_c.at[place, i, :, cut] for i in range(2)]
                 self.terms = [ref.at[l, lane, chip, :, cols] for ref in (own_gu, sib_gu)]
                 self.result = [out.at[l, :, cols] for out in (dg_out, du_out)]
@@ -406,37 +420,41 @@
             pairs = zip(self.terms, self.st)
             return [pltpu.make_async_copy(a, b, st_sem.at[self.place, i]) for i, (a, b) in enumerate(pairs)]
 
-        def send(self, to):
+        def send(self, to, piece):
             recv, sent = self.sems
-            return remote(self.slots[0], self.slots[to], sent.at[self.s], recv.at[self.s + to], here.next)
+            src, dst = self.slots[piece][0], self.slots[piece][to]
+            return remote(src, dst, sent.at[self.s, piece], recv.at[self.s + to, piece], here.next)
 
         def finish(self, action):
             if not isinstance(self.result, list):
-                action(pltpu.make_async_copy(self.slots[0], self.result, self.fin))
+                action(pltpu.make_async_copy(self.slot, self.result, self.fin))
                 return
             for lane, result in enumerate(self.result):
-                copy = pltpu.make_async_copy(self.slots[0], result, self.fin)
+                copy = pltpu.make_async_copy(self.slot, result, self.fin)
                 pl.when(self.lane == lane)(functools.partial(action, copy))
 
         def step(self):
             wait(self.stage())
-            slot = self.slots[0]
-            ends = [st[...].astype(F32) for st in self.st]
-
-            @pl.when(self.s > 0)
-            def _():
-                self.send(0).wait_recv()
-                slot[...] = (slot[...].astype(F32) + (ends[0] + ends[1])).astype(BF16)
-
-            @pl.when(self.s == 0)
-            def _():
-                slot[...] = (ends[0] + ends[1]).astype(BF16)
-
-            pl.when(self.s < STEPS - 1)(lambda: self.send(1).start())
+            for i in range(2):
+                slot = self.slots[i][0]
+                own, sib = (end[...].astype(F32) for end in self.ends[i])
+                total = own + sib
+
+                @pl.when(self.s > 0)
+                def _():
+                    self.send(0, i).wait_recv()
+                    slot[...] = (slot[...].astype(F32) + total).astype(BF16)
+
+                @pl.when(self.s == 0)
+                def _():
+                    slot[...] = total.astype(BF16)
+
+                pl.when(self.s < STEPS - 1)(lambda: self.send(1, i).start())
             pl.when(self.s == STEPS - 1)(lambda: self.finish(lambda copy: copy.start()))
 
         def wait_out(self):
-            pl.when(self.s < STEPS - 1)(lambda: self.send(1).wait_send())
+            for i in range(2):
+                pl.when(self.s < STEPS - 1)(lambda: self.send(1, i).wait_send())
             pl.when(self.s == STEPS - 1)(lambda: self.finish(lambda copy: copy.wait()))
 
         def prefetch(self):
@@ -553,16 +571,18 @@
         load_at.start()
         pl.when(i == 0)(pltpu.make_async_copy(h1_ref, h_s, misc_sem.at[1]).start)
         pl.when(i == 1)(pltpu.make_async_copy(x_ref, h_s, misc_sem.at[1]).start)
-        start(lhs_loads(l, 0, 0))
+        for s in range(2):
+            start(lhs_loads(l, s, s))
         first_loads = lambda: both_halves(0, lambda half: start(tile_loads(l, 0, 0, half)))
         pl.when(i == 1)(first_loads)
 
         def pair(s):
             slot = lax.rem(s, 2)
-            pl.when(s < STEPS - 1)(lambda: start(lhs_loads(l, s + 1, 1 - slot)))
-            wait(lhs_loads(l, s, slot))
+            there = lax.rem(s, 3)
+            pl.when(s < STEPS - 2)(lambda: start(lhs_loads(l, s + 2, lax.rem(s + 2, 3))))
+            wait(lhs_loads(l, s, there))
             for b in range(2):
-                blk_s[slot, b] = dot(lhs_t[slot, b], dh_s[...]).astype(BF16)
+                blk_s[slot, b] = dot(lhs_t[there, b], dh_s[...]).astype(BF16)
             start(block_copies(l, s, slot))
 
             @pl.when(i == 0)
@@ -680,6 +700,7 @@
         vmem((T, FFP), BF16),
         vmem((FFP, D), BF16),
         vmem((2, D, 2 * TILE), BF16),
+        vmem((2, ROWS, 2 * TILE), F32),
         vmem((2, T, TILE), F32),
         vmem((2, T, TILE), F32),
         vmem((2, TILE, T), BF16),
@@ -695,7 +716,7 @@
         vmem((D, T), BF16),
         vmem((T, D), BF16),
         vmem((T, D), F32),
-        vmem((*two, RD, T), BF16),
+        vmem((3, 2, RD, T), BF16),
         vmem((*two, RD, D), BF16),
         vmem((2, D, 2 * BIG), BF16),
         vmem((2, BIG, D), BF16),
@@ -732,13 +753,12 @@
     gather_sems = [dma((UNITS, HOPS, ITEMS)), dma((UNITS, HOPS)), *[dma((UNITS,))] * 4]
     forward_sems = [dma((LAYERS * 6,)), dma(two), dma((2, 3)), dma((2,)), dma((2,))]
     backward_sems = [
-        dma((*per_part, STEPS)),
-        dma((*per_part, STEPS)),
+        *[dma((*per_part, STEPS, 2))] * 2,
         dma((PLACES, 2)),
         dma(per_part),
         dma((LAYERS, STEPS)),
         dma((LAYERS, PAIRS - 1)),
-        dma(two),
+        dma((3, 2)),
         dma((2,)),
         dma((2,)),
         dma((*two, 5)),

time: 497 us -> 484 us (0.974)
  Pallas kernels: 489 us -> 477 us
    pallas_call x1, Pallas kernels: 489 us -> 477 us  [both_passes(): pl.pallas_call(kernel, out_shape=outs, in_specs=[any_] * 2 + [vmem] * 3,...]
where the time goes in v3:
time: 484 us
  Pallas kernels  477 us (99%)
  local copies, waits for them, and re-layouts  6.53 us (1%)
    pallas_call x1, Pallas kernels, both_passes(): pl.pallas_call(kernel, out_shape=outs, in_specs=[any_] * 2 + [vmem] * 3,...  477 us

profile of v3, /device:TPU:0, one launch (start us, length us, event | category | flops | bytes accessed | tf_op | source)
XLA Modules:
  0.0 483.8 jit_solution(10908409309293905676)
XLA Ops:
  0.6 476.6 %both_passes.1 = (bf16[1024,896]{1,0:T(8,128)(2,1)}, bf16[2,56,4736]{2,1,0:T(8,128)(2,1)}, bf16[2,56,4736]{2,1,0:T(8,128)(2,1)}, bf16[2,296,896]{2,1,0:T(8,128)(...) custom-call(bf16[1024,896]{1,0:T(8,128)(2,1)} %bitcast.4, ...), custom_call_target="tpu_custom_call" | custom-call | tf_op jit(solution)/shard_map/both_passes/pallas_call | solution.py:769
  477.3 0.0 copy-start.2
  477.3 3.0 copy.13
  480.2 0.0 copy-done.2
  480.2 0.0 copy-start.1
  480.2 0.0 copy-start
  480.2 1.0 copy.14
  481.2 0.6 copy-done.1
  481.8 1.0 copy.15
  482.8 0.0 copy-done
  482.8 1.0 copy.16
Async XLA Ops:
  477.3 3.0 copy-start.2
  480.2 1.6 copy-start.1
  480.2 2.6 copy-start

commit v4 on v3

--- a/solution.py
+++ b/solution.py
@@ -381,7 +381,7 @@
 
 def backward_pass(
     here, gather, dy_ref, x_ref, h1_ref, g_ref, d_ref, p_ref, q_ref, actt_ref, at_ref,
-    dx_out, dg_out, du_out, dd_out, own_gu, sib_gu, own_d, sib_d, slot_d, slot_c,
+    dx_out, dg_out, du_out, dd_out, terms_gu, terms_d, slot_d, slot_c,
     red_recv, red_send, st_sem, fin_sem, sd_recv, sgu_recv, lhs_sem, blk_sem, blk_send, w_sem, term_sem, term_send, misc_sem,
     dh_s, at_s, h_s, dacc, lhs_t, blk_s, wgu_t, wd_t, p_t, q_t, dz_s, term_s, st_d, st_c,
 ):
@@ -401,8 +401,8 @@
                 self.slot = slot_d.at[lane, s, cut, :]
                 self.slots = [[slot_d.at[lane, to, piece, :] for to in (s, s + 1)] for piece in pieces]
                 self.ends = [[st_d.at[place, i, piece, :] for i in range(2)] for piece in pieces]
-                self.st = [st_d.at[place, i, cut, :] for i in range(2)]
-                self.terms = [ref.at[l, chip, rows, :] for ref in (own_d, sib_d)]
+                self.terms = terms_d.at[:, l, chip, rows, :]
+                self.st = st_d.at[place, :, cut, :]
                 self.result = dd_out.at[l, rows, :]
             else:
                 part = pair - 1
@@ -412,18 +412,17 @@
                 self.slot = slot_c.at[part, lane, s, :, cut]
                 self.slots = [[slot_c.at[part, lane, to, :, piece] for to in (s, s + 1)] for piece in pieces]
                 self.ends = [[st_c.at[place, i, :, piece] for i in range(2)] for piece in pieces]
-                self.st = [st_c.at[place, i, :, cut] for i in range(2)]
-                self.terms = [ref.at[l, lane, chip, :, cols] for ref in (own_gu, sib_gu)]
+                self.terms = terms_gu.at[:, l, lane, chip, :, cols]
+                self.st = st_c.at[place, :, :, cut]
                 self.result = [out.at[l, :, cols] for out in (dg_out, du_out)]
 
         def stage(self):
-            pairs = zip(self.terms, self.st)
-            return [pltpu.make_async_copy(a, b, st_sem.at[self.place, i]) for i, (a, b) in enumerate(pairs)]
+            return pltpu.make_async_copy(self.terms, self.st, st_sem.at[self.place])
 
         def send(self, to, piece):
             recv, sent = self.sems
             src, dst = self.slots[piece][0], self.slots[piece][to]
-            return remote(src, dst, sent.at[self.s, piece], recv.at[self.s + to, piece], here.next)
+            return remote(src, dst, sent.at[self.s], recv.at[self.s + to, piece], here.next)
 
         def finish(self, action):
             if not isinstance(self.result, list):
@@ -434,7 +433,7 @@
                 pl.when(self.lane == lane)(functools.partial(action, copy))
 
         def step(self):
-            wait(self.stage())
+            self.stage().wait()
             for i in range(2):
                 slot = self.slots[i][0]
                 own, sib = (end[...].astype(F32) for end in self.ends[i])
@@ -453,12 +452,13 @@
             pl.when(self.s == STEPS - 1)(lambda: self.finish(lambda copy: copy.start()))
 
         def wait_out(self):
-            for i in range(2):
-                pl.when(self.s < STEPS - 1)(lambda: self.send(1, i).wait_send())
+            recv, sent = self.sems
+            both = remote(self.slot, self.slot, sent.at[self.s], recv.at[self.s, 0], here.next)
+            pl.when(self.s < STEPS - 1)(both.wait_send)
             pl.when(self.s == STEPS - 1)(lambda: self.finish(lambda copy: copy.wait()))
 
         def prefetch(self):
-            start(self.stage())
+            self.stage().start()
 
     def with_lane(e, action, ahead_of=lambda l, pair, lane, s: None):
         round_, place = e // PLACES, lax.rem(e, PLACES)
@@ -482,7 +482,7 @@
     def terms_ready(l, pair, lane, s):
         @pl.when((pair == 0) & (lane == 0))
         def _():
-            whole = sib_d.at[l, 0]
+            whole = terms_d.at[1, l, 0]
             remote(whole, whole, blk_send.at[0], sd_recv.at[l, s], here.sibling).wait_recv()
 
         @pl.when((pair > 0) & (lane == 0) & (s == 0))
@@ -492,7 +492,7 @@
 
                 @pl.when((pair == PAIRS - 1) == is_last)
                 def _(width=width):
-                    part = sib_gu.at[l, :, :, :, pl.ds(0, width)]
+                    part = terms_gu.at[1, l, :, :, :, pl.ds(0, width)]
                     sem = sgu_recv.at[l, pair - 1]
                     remote(part, part, term_send.at[0, 0], sem, here.sibling).wait_recv()
 
@@ -518,8 +518,8 @@
     def block_copies(l, s, slot):
         mine, other = chips(s)
         return (
-            pltpu.make_async_copy(blk_s.at[slot, 0], own_d.at[l, mine], blk_sem.at[slot]),
-            remote(blk_s.at[slot, 1], sib_d.at[l, other], blk_send.at[slot], sd_recv.at[l, s], here.sibling),
+            pltpu.make_async_copy(blk_s.at[slot, 0], terms_d.at[0, l, mine], blk_sem.at[slot]),
+            remote(blk_s.at[slot, 1], terms_d.at[1, l, other], blk_send.at[slot], sd_recv.at[l, s], here.sibling),
         )
 
     def both_halves(j, action):
@@ -544,8 +544,8 @@
         own, sib = [], []
         for m in range(2):
             mine, other = term_s.at[half, m, :, here.core], term_s.at[half, m, :, 1 - here.core]
-            own.append(pltpu.make_async_copy(mine, own_gu.at[l, m, :, :, cols], term_sem.at[half, m]))
-            to = sib_gu.at[l, m, :, :, cols]
+            own.append(pltpu.make_async_copy(mine, terms_gu.at[0, l, m, :, :, cols], term_sem.at[half, m]))
+            to = terms_gu.at[1, l, m, :, :, cols]
             sib.append(remote(other, to, term_send.at[half, m], sgu_recv.at[l, part], here.sibling))
         return own, sib
 
@@ -681,7 +681,7 @@
 
 def kernel(
     dy_ref, x_ref, wg_ref, wu_ref, wd_ref,
-    dx_out, dg_out, du_out, dd_out, own_gu, sib_gu, own_d, sib_d, g_out, d_out, p_out, q_out, actt_out, at_out, h1_out,
+    dx_out, dg_out, du_out, dd_out, terms_gu, terms_d, g_out, d_out, p_out, q_out, actt_out, at_out, h1_out,
     slot_d, slot_c, *sems,
 ):
     gather_sems, forward_sems, backward_sems = sems[:6], sems[6:11], sems[11:]
@@ -710,7 +710,7 @@
     pl.run_scoped(
         functools.partial(
             backward_pass, here, gather, dy_ref, x_ref, h1_out, g_out, d_out, p_out, q_out, actt_out, at_out,
-            dx_out, dg_out, du_out, dd_out, own_gu, sib_gu, own_d, sib_d, slot_d, slot_c, *backward_sems,
+            dx_out, dg_out, du_out, dd_out, terms_gu, terms_d, slot_d, slot_c, *backward_sems,
         ),
         vmem((T, D), BF16),
         vmem((D, T), BF16),
@@ -741,8 +741,8 @@
         shape((T, D), BF16),
         *[shape((LAYERS, RG, FF), BF16)] * 2,
         shape((LAYERS, RD, D), BF16),
-        *[shape((LAYERS, 2, 8, RG, FFP), BF16)] * 2,
-        *[shape((LAYERS, 8, RD, D), BF16)] * 2,
+        shape((2, LAYERS, 2, 8, RG, FFP), BF16),
+        shape((2, LAYERS, 8, RD, D), BF16),
         shape((LAYERS, 2, D, FFP), BF16),
         shape((LAYERS, FFP, D), BF16),
         *[shape((LAYERS, TILES, T, TILE), F32)] * 2,
@@ -753,8 +753,9 @@
     gather_sems = [dma((UNITS, HOPS, ITEMS)), dma((UNITS, HOPS)), *[dma((UNITS,))] * 4]
     forward_sems = [dma((LAYERS * 6,)), dma(two), dma((2, 3)), dma((2,)), dma((2,))]
     backward_sems = [
-        *[dma((*per_part, STEPS, 2))] * 2,
-        dma((PLACES, 2)),
+        dma((*per_part, STEPS, 2)),
+        dma((*per_part, STEPS)),
+        dma((PLACES,)),
         dma(per_part),
         dma((LAYERS, STEPS)),
         dma((LAYERS, PAIRS - 1)),

time: 484 us -> 483 us (level)
  no operation moved by 1% of the time
where the time goes in v4:
time: 483 us
  Pallas kernels  476 us (99%)
  local copies, waits for them, and re-layouts  6.53 us (1%)
    pallas_call x1, Pallas kernels, both_passes(): pl.pallas_call(kernel, out_shape=outs, in_specs=[any_] * 2 + [vmem] * 3,...  476 us

profile of v4, /device:TPU:0, one launch (start us, length us, event | category | flops | bytes accessed | tf_op | source)
XLA Modules:
  0.0 482.8 jit_solution(16152538515089566300)
XLA Ops:
  0.6 475.6 %both_passes.1 = (bf16[1024,896]{1,0:T(8,128)(2,1)}, bf16[2,56,4736]{2,1,0:T(8,128)(2,1)}, bf16[2,56,4736]{2,1,0:T(8,128)(2,1)}, bf16[2,296,896]{2,1,0:T(8,128)(...) custom-call(bf16[1024,896]{1,0:T(8,128)(2,1)} %bitcast.4, ...), custom_call_target="tpu_custom_call" | custom-call | tf_op jit(solution)/shard_map/both_passes/pallas_call | solution.py:770
  476.3 0.0 copy-start.2
  476.3 3.0 copy.13
  479.3 0.0 copy-done.2
  479.3 0.0 copy-start.1
  479.3 0.0 copy-start
  479.3 1.0 copy.14
  480.2 0.6 copy-done.1
  480.9 1.0 copy.15
  481.8 0.0 copy-done
  481.9 1.0 copy.16
Async XLA Ops:
  476.3 3.0 copy-start.2
  479.3 1.6 copy-start.1
  479.3 2.6 copy-start
